TPU v7x, 8 devices: a whole 2x2x1 slice. The times are simulated.
8 devices in a mesh: fsdp: 8 (over z, y, x, core).
Axes of the slice: x: 2, y: 2, z: 1, core: 2. Of those that a mesh axis runs over, the one named last changes fastest.
Arguments:
- tok_ids: int32 [16, 1024], P('fsdp')
- grad_out: bfloat16 [16, 1024, 1536], P('fsdp')
- emb_table: bfloat16 [151936, 1536], P('fsdp')
- norm_gain: bfloat16 [1536], P('fsdp')
- w_query: bfloat16 [1536, 1536], P('fsdp')
- b_query: bfloat16 [1536], P('fsdp')
- w_key: bfloat16 [1536, 256], P('fsdp')
- b_key: bfloat16 [256], P('fsdp')
- w_value: bfloat16 [1536, 256], P('fsdp')
- b_value: bfloat16 [256], P('fsdp')
- w_out: bfloat16 [1536, 1536], P('fsdp')
Outputs:
- output 1: bfloat16 [16, 1024, 1536], P('fsdp')
- output 2: bfloat16 [151936, 1536], P('fsdp')
- output 3: float32 [1536], P('fsdp')
- output 4: float32 [1536, 1536], P('fsdp')
- output 5: float32 [1536], P('fsdp')
- output 6: float32 [1536, 256], P('fsdp')
- output 7: float32 [256], P('fsdp')
- output 8: float32 [1536, 256], P('fsdp')
- output 9: float32 [256], P('fsdp')
- output 10: float32 [1536, 1536], P('fsdp')
All inputs are finite; a program needn't handle non-finite values.
Results may differ from a plain program's by a relative error of at most 0.0157803.
Values are sent between devices in bfloat16 or wider.
A program may use at most 1 GiB of HBM per device.

v0:
```python
import jax
import jax.numpy as jnp
from jax import lax
from jax.sharding import PartitionSpec as P

HEAD_DIM = 128
ROPE_THETA = 1.0e6
NORM_EPS = 1e-6
MASK_VALUE = -1e30


def rope_tables(seq_len):
    half_dim = HEAD_DIM // 2
    inv_freq = jnp.power(ROPE_THETA, -(jnp.arange(half_dim, dtype=jnp.float32) * 2.0 / HEAD_DIM))
    angles = jnp.arange(seq_len, dtype=jnp.float32)[:, None] * inv_freq[None, :]
    angles = jnp.concatenate([angles, angles], axis=-1)
    return jnp.cos(angles)[:, None, :], jnp.sin(angles)[:, None, :]


def rotate(vector, cos_t, sin_t):
    half_dim = HEAD_DIM // 2
    turned = jnp.concatenate([-vector[..., half_dim:], vector[..., :half_dim]], axis=-1)
    return vector * cos_t + turned * sin_t


def rotate_back(grad_in, cos_t, sin_t):
    half_dim = HEAD_DIM // 2
    scaled = grad_in * sin_t
    turned = jnp.concatenate([scaled[..., half_dim:], -scaled[..., :half_dim]], axis=-1)
    return grad_in * cos_t + turned


def block_fwd_bwd(x_rows, grad_out, gain_vec, w_query, b_query, w_key, b_key, w_value, b_value, w_out):
    batch_size, seq_len, model_width = x_rows.shape
    n_heads = w_query.shape[1] // HEAD_DIM
    kv_heads = w_key.shape[1] // HEAD_DIM
    q_group = n_heads // kv_heads
    score_scale = HEAD_DIM ** -0.5
    cos_t, sin_t = rope_tables(seq_len)
    x_full = x_rows.astype(jnp.float32)
    inv_rms = lax.rsqrt(jnp.mean(x_full * x_full, axis=-1, keepdims=True) + NORM_EPS)
    x_norm = x_full * inv_rms
    gain_f = gain_vec.astype(jnp.float32)
    hidden = (x_norm * gain_f).astype(jnp.bfloat16)
    q_lin = jnp.einsum("bli,io->blo", hidden, w_query, preferred_element_type=jnp.float32) + b_query.astype(jnp.float32)
    k_lin = jnp.einsum("bli,io->blo", hidden, w_key, preferred_element_type=jnp.float32) + b_key.astype(jnp.float32)
    v_lin = jnp.einsum("bli,io->blo", hidden, w_value, preferred_element_type=jnp.float32) + b_value.astype(jnp.float32)
    q_rot = rotate(q_lin.reshape(batch_size, seq_len, n_heads, HEAD_DIM), cos_t, sin_t).astype(jnp.bfloat16)
    q_rot = q_rot.reshape(batch_size, seq_len, kv_heads, q_group, HEAD_DIM)
    k_rot = rotate(k_lin.reshape(batch_size, seq_len, kv_heads, HEAD_DIM), cos_t, sin_t).astype(jnp.bfloat16)
    v_val = v_lin.astype(jnp.bfloat16).reshape(batch_size, seq_len, kv_heads, HEAD_DIM)
    scores = jnp.einsum("bqkgd,bskd->bkgqs", q_rot, k_rot, preferred_element_type=jnp.float32) * score_scale
    causal = jnp.arange(seq_len)[:, None] >= jnp.arange(seq_len)[None, :]
    scores = jnp.where(causal, scores, MASK_VALUE)
    prob_f = jax.nn.softmax(scores, axis=-1)
    prob_b = prob_f.astype(jnp.bfloat16)
    attn_out = jnp.einsum("bkgqs,bskd->bqkgd", prob_b, v_val, preferred_element_type=jnp.float32)
    attn_b = attn_out.astype(jnp.bfloat16).reshape(batch_size, seq_len, n_heads * HEAD_DIM)
    proj_out = jnp.einsum("bli,io->blo", attn_b, w_out, preferred_element_type=jnp.float32)
    block_out = (x_full + proj_out).astype(jnp.bfloat16)

    grad_wo = jnp.einsum("bli,blo->io", attn_b, grad_out, preferred_element_type=jnp.float32)
    d_attn = jnp.einsum("blo,io->bli", grad_out, w_out, preferred_element_type=jnp.float32)
    d_attn = d_attn.astype(jnp.bfloat16).reshape(batch_size, seq_len, kv_heads, q_group, HEAD_DIM)
    d_probs = jnp.einsum("bqkgd,bskd->bkgqs", d_attn, v_val, preferred_element_type=jnp.float32)
    d_val = jnp.einsum("bkgqs,bqkgd->bskd", prob_b, d_attn, preferred_element_type=jnp.float32)
    d_scores = prob_f * (d_probs - jnp.sum(d_probs * prob_f, axis=-1, keepdims=True))
    d_scores = (d_scores * score_scale).astype(jnp.bfloat16)
    d_qrot = jnp.einsum("bkgqs,bskd->bqkgd", d_scores, k_rot, preferred_element_type=jnp.float32)
    d_krot = jnp.einsum("bkgqs,bqkgd->bskd", d_scores, q_rot, preferred_element_type=jnp.float32)
    d_query = rotate_back(d_qrot.reshape(batch_size, seq_len, n_heads, HEAD_DIM), cos_t, sin_t)
    d_query = d_query.reshape(batch_size, seq_len, n_heads * HEAD_DIM)
    d_key = rotate_back(d_krot, cos_t, sin_t).reshape(batch_size, seq_len, kv_heads * HEAD_DIM)
    d_value = d_val.reshape(batch_size, seq_len, kv_heads * HEAD_DIM)
    grad_bq = jnp.sum(d_query, axis=(0, 1))
    grad_bk = jnp.sum(d_key, axis=(0, 1))
    grad_bv = jnp.sum(d_value, axis=(0, 1))
    dq_b = d_query.astype(jnp.bfloat16)
    dk_b = d_key.astype(jnp.bfloat16)
    dv_b = d_value.astype(jnp.bfloat16)
    grad_wq = jnp.einsum("bli,blo->io", hidden, dq_b, preferred_element_type=jnp.float32)
    grad_wk = jnp.einsum("bli,blo->io", hidden, dk_b, preferred_element_type=jnp.float32)
    grad_wv = jnp.einsum("bli,blo->io", hidden, dv_b, preferred_element_type=jnp.float32)
    d_hidden = jnp.einsum("blo,io->bli", dq_b, w_query, preferred_element_type=jnp.float32)
    d_hidden = d_hidden + jnp.einsum("blo,io->bli", dk_b, w_key, preferred_element_type=jnp.float32)
    d_hidden = d_hidden + jnp.einsum("blo,io->bli", dv_b, w_value, preferred_element_type=jnp.float32)
    grad_gain = jnp.sum(d_hidden * x_norm, axis=(0, 1))
    d_norm = d_hidden * gain_f
    d_x = grad_out.astype(jnp.float32) + inv_rms * (d_norm - x_norm * jnp.mean(d_norm * x_norm, axis=-1, keepdims=True))
    return block_out, d_x, (grad_gain, grad_wq, grad_bq, grad_wk, grad_bk, grad_wv, grad_bv, grad_wo)


def solution(mesh):
    row_spec = P("fsdp", None)
    vec_spec = P("fsdp")
    act_spec = P("fsdp", None, None)
    weight_specs = (vec_spec, row_spec, vec_spec, row_spec, vec_spec, row_spec, vec_spec, row_spec)
    in_specs = (row_spec, act_spec, row_spec) + weight_specs
    out_specs = (act_spec, row_spec) + weight_specs

    def device_step(tok_ids, grad_out, table_part, gain_part, wq_part, bq_part, wk_part, bk_part, wv_part, bv_part, wo_part):
        rows_dev = table_part.shape[0]
        model_width = table_part.shape[1]
        first_row = lax.axis_index("fsdp") * rows_dev
        all_ids = lax.all_gather(tok_ids, "fsdp")
        local_idx = all_ids - first_row
        is_owned = (local_idx >= 0) & (local_idx < rows_dev)
        looked = jnp.take(table_part, jnp.where(is_owned, local_idx, 0), axis=0)
        looked = jnp.where(is_owned[..., None], looked, jnp.zeros((), jnp.bfloat16))
        x_rows = lax.psum_scatter(looked, "fsdp", scatter_dimension=0)
        gain_full = lax.all_gather(gain_part, "fsdp", axis=0, tiled=True)
        wq_full = lax.all_gather(wq_part, "fsdp", axis=0, tiled=True)
        bq_full = lax.all_gather(bq_part, "fsdp", axis=0, tiled=True)
        wk_full = lax.all_gather(wk_part, "fsdp", axis=0, tiled=True)
        bk_full = lax.all_gather(bk_part, "fsdp", axis=0, tiled=True)
        wv_full = lax.all_gather(wv_part, "fsdp", axis=0, tiled=True)
        bv_full = lax.all_gather(bv_part, "fsdp", axis=0, tiled=True)
        wo_full = lax.all_gather(wo_part, "fsdp", axis=0, tiled=True)
        block_out, d_x, grad_list = block_fwd_bwd(x_rows, grad_out, gain_full, wq_full, bq_full, wk_full, bk_full, wv_full, bv_full, wo_full)
        all_dx = lax.all_gather(d_x, "fsdp")
        seg_idx = jnp.where(is_owned, local_idx, rows_dev)
        grad_part = jax.ops.segment_sum(all_dx.reshape(-1, model_width), seg_idx.reshape(-1), num_segments=rows_dev)
        reduced = tuple(lax.psum_scatter(grad_full, "fsdp", scatter_dimension=0, tiled=True) for grad_full in grad_list)
        return (block_out, grad_part.astype(jnp.bfloat16)) + reduced

    return jax.shard_map(device_step, mesh=mesh, in_specs=in_specs, out_specs=out_specs, check_vma=False)
```

profile of v0, /device:TPU:0, one launch (start us, length us, event | category | flops | bytes accessed | tf_op | source)
XLA Modules:
  0.0 2615.7 jit_solution(1653434611733396538)
XLA Ops:
  7.2 0.7 all-gather.9.cloned.1.call-update
  8.0 14.2 all-gather.2
  22.2 0.7 select_bitcast_fusion
  22.9 548.8 %gather_fusion = bf16[16384,1536]{1,0:T(8,128)(2,1)} fusion(bf16[18992,1536]{1,0:T(8,128)(2,1)} %param.13, s32[16384]{0:T(1024)S(1)} %broadcast_clamp_fusion.1), kind=kCustom, calls=%fused_computation | custom fusion | bytes 100728832 | tf_op jit(solution)/shard_map/jit(_take)/gather | solution.py:108
  571.9 33.7 %select_select_fusion = bf16[8,2,1024,1536]{3,2,1,0:T(8,128)(2,1)} fusion(bf16[8,2,1024,1536]{3,2,1,0:T(8,128)(2,1)} %bitcast.213, pred[8,2,1024]{2,1,0:T(4,128)(4,1)S(1)} %get-tuple-element.39, pred[8,2,1024]{2,1,0:T(4,128)(4,1)S(1)} %get-tuple-element.38), kind=kLoop, calls=%fused_computation.19 | loop fusion | flops 50331648 | bytes 100696064 | tf_op jit(solution)/shard_map/jit(_where)/select_n | solution.py:109
  605.7 0.7 all-gather.7.cloned.1.call-update
  606.5 0.2 dynamic-update-slice.1
  606.8 0.2 dynamic-update-slice.2
  607.0 0.2 dynamic-update-slice
  607.3 0.2 dynamic-update-slice.3
  607.5 294.2 %all-reduce.9 = (bf16[1536]{0:T(1024)(128)(2,1)S(1)}, bf16[256]{0:T(256)(128)(2,1)S(1)}, bf16[256]{0:T(256)(128)(2,1)S(1)}, bf16[1536]{0:T(1024)(128)(2,1)S(1)}) all-reduce(bf16[1536]{0:T(1024)(128)(2,1)S(1)} %dynamic-update-slice, bf16[256]{0:T(256)(128)(2,1)S(1)} %dynamic-update-slice.1, ...), channel_id=1, replica_groups=mesh['fsdp'=8] {'fsdp'}, use_global_device_ids=true, to_apply=%add | all-reduce | flops 3584 | bytes 14336
  901.9 2.7 fusion.85
  904.6 13.9 all_gather.41
  918.5 13.6 all_gather.39
  932.1 1.3 iota_compare_fusion
  933.3 15.1 convolution_convert_fusion
  948.5 8.6 copy.72
  957.1 195.1 %reduce-scatter.6.cloned.1.call-done = bf16[1,2,1024,1536]{3,2,1,0:T(8,128)(2,1)} async-done(((bf16[8,2,1024,1536]{3,2,1,0:T(8,128)(2,1)}), bf16[1,2,1024,1536]{3,2,1,0:T(8,128)(2,1)}) %reduce-scatter.6.cloned.1.call-update) | async-done | bytes 6291472 | tf_op jit(solution)/shard_map/reduce_scatter | solution.py:110
  1152.2 4.1 fusion.35
  1156.3 4.4 fusion.75
  1160.7 1.3 copy-done.5
  1162.0 1.5 slice_negate_fusion.3
  1163.5 23.5 all-gather.7.cloned.1.call-done
  1187.0 16.2 broadcast_add_fusion
  1203.2 12.8 copy.66
  1215.9 12.4 slice_negate_fusion.1
  1228.4 5.0 add_convert_fusion.1
  1233.4 37.5 %fusion.98 = f32[2,2,1024,1024,6]{3,2,4,1,0:T(8,128)} fusion(bf16[2,1024,2,128,1]{1,3,4,2,0:T(8,128)(2,1)} %bitcast.232, bf16[2,1024,2,6,128]{1,4,3,2,0:T(8,128)(2,1)} %bitcast.222), kind=kOutput, calls=%fused_computation.124 | convolution fusion | flops 6442450944 | bytes 108003328 | tf_op jit(solution)/shard_map/bqkgd,bskd->bkgqs/dot_general | solution.py:65
  1271.0 3.1 fusion.78
  1274.2 13.1 fusion.40
  1287.3 46.1 %fusion.97 = (f32[2,2,6,1024]{3,2,1,0:T(8,128)S(1)}, f32[2,2,6,1024,1024]{3,4,2,1,0:T(8,128)}) fusion(pred[1024,1024]{0,1:T(8,128)(4,1)S(1)} %copy-done.15, bf16[2,1024,2,128,1]{1,3,4,2,0:T(8,128)(2,1)S(1)} %copy-done.16, bf16[2,1024,2,6,128]{1,4,3,2,0:T(8,128)(2,1)} %fusion.40), kind=kOutput, calls=%fused_computation.123 | convolution fusion | flops 6543115264 | bytes 109150208 | tf_op jit(solution)/shard_map/sub | solution.py:55
  1333.4 36.8 %bitcast_convert_fusion = (bf16[2,1024,2,128]{1,3,2,0:T(8,128)(2,1)}, f32[2,2,128,1024,1]{3,2,4,1,0:T(8,128)}) fusion(bf16[2,1024,2,6,128]{1,4,3,2,0:T(8,128)(2,1)} %bitcast.223, f32[2,2,6,1024,1024]{3,4,2,1,0:T(8,128)} %get-tuple-element.41, f32[2,2,6,1024]{3,2,1,0:T(8,128)S(1)} %get-tuple-element.40), kind=kOutput, calls=%fused_computation.86 | convolution fusion | flops 6493306880 | bytes 110198784 | tf_op jit(solution)/shard_map/bkgqs,bqkgd->bskd/dot_general | solution.py:66
  1370.2 125.9 %bitcast_multiply_fusion.10 = (f32[2,1024,2,128]{1,3,2,0:T(8,128)}, f32[2,2,128,1024,1]{3,2,4,1,0:T(8,128)}) fusion(f32[1024,128]{0,1:T(8,128)S(1)} %copy-done.4, bf16[2,1024,2,6,128]{1,4,3,2,0:T(8,128)(2,1)} %fusion.40, f32[2,2,1024,1024,6]{3,2,4,1,0:T(8,128)} %fusion.98, f32[2,2,6,1024,1024]{3,4,2,1,0:T(8,128)} %get-tuple-element.41, ...), kind=kOutput, calls=%fused_computation.87 | convolution fusion | flops 6619161600 | bytes 212434944 | tf_op jit(solution)/shard_map/bkgqs,bqkgd->bskd/dot_general | solution.py:70
  1496.1 124.1 %fusion.17 = f32[2,2,128,6,1024]{4,2,3,1,0:T(8,128)} fusion(bf16[2,1024,2,128,1]{1,3,4,2,0:T(8,128)(2,1)S(1)} %copy-done.17, f32[2,2,1024,1024,6]{3,2,4,1,0:T(8,128)} %fusion.98, f32[2,2,6,1024,1024]{3,4,2,1,0:T(8,128)} %get-tuple-element.41, f32[2,2,6,1024]{3,2,1,0:T(8,128)S(1)} %get-tuple-element.40), kind=kOutput, calls=%fused_computation.23 | convolution fusion | flops 6618637312 | bytes 215056384 | tf_op jit(solution)/shard_map/bkgqs,bskd->bqkgd/dot_general | solution.py:69
  1620.2 1.7 fusion.96
  1621.9 2.5 fusion.86
  1624.4 1.0 copy-done.7
  1625.4 6.4 fusion.79
  1631.8 12.1 broadcast_multiply_fusion
  1643.9 12.4 fusion.95
  1656.3 18.2 add_convert_fusion
  1674.5 0.8 mul.208
  1675.3 9.8 fusion.43
  1685.1 16.6 fusion.49
  1701.7 14.6 fusion.34
  1716.3 13.2 fusion.33
  1729.6 1.1 copy-done.14
  1730.8 6.3 fusion.68
  1737.1 0.4 reduce-scatter.10.cloned.1.call-start
  1737.6 6.3 fusion.65
  1744.0 34.8 %fusion.52 = bf16[2,2,128,6,1024]{4,2,3,1,0:T(8,128)(2,1)} fusion(bf16[2,1024,2,128,1]{1,3,4,2,0:T(8,128)(2,1)S(1)} %bitcast.233, f32[2,2,6,1024,1024]{3,4,2,1,0:T(8,128)} %get-tuple-element.41, f32[2,2,6,1024]{3,2,1,0:T(8,128)S(1)} %get-tuple-element.40), kind=kOutput, calls=%fused_computation.74 | convolution fusion | flops 6495928320 | bytes 108101632 | tf_op jit(solution)/shard_map/bkgqs,bskd->bqkgd/dot_general | solution.py:57
  1778.8 15.5 convolution_bitcast_fusion.1
  1794.6 17.0 convolution_bitcast_fusion
  1811.7 7.1 sort
  1818.9 9.1 fusion.41
  1828.2 23.4 all-reduce.8
  1851.6 0.6 dynamic-slice
  1852.2 0.6 dynamic-slice.1
  1852.9 0.6 dynamic-slice.2
  1853.5 0.6 dynamic-slice.3
  1854.1 16.1 fusion.36
  1870.2 300.2 %all-gather.11.cloned.1.call-done = f32[16,1024,1536]{2,1,0:T(8,128)} async-done(((f32[2,1024,1536]{2,1,0:T(8,128)}), f32[16,1024,1536]{2,1,0:T(8,128)}) %all-gather.11.cloned.1.call-update) | async-done | bytes 100663312 | tf_op jit(solution)/shard_map/all_gather | solution.py:120
  2170.3 382.6 %scatter_custom_fusion = f32[18992,1536]{1,0:T(8,128)} fusion(s32[16384]{0:T(1024)S(1)} %get-tuple-element.10, f32[16384,1536]{1,0:T(8,128)} %bitcast.38, s32[16384]{0:T(1024)S(1)} %broadcast_clamp_fusion, f32[]{:T(128)} %constant.20.clone.1), kind=kCustom, calls=%fused_computation.5 | custom fusion | flops 25165824 | bytes 116687360 | tf_op jit(solution)/shard_map/scatter-add | solution.py:122
  2552.9 55.4 %convert_element_type.117 = bf16[18992,1536]{1,0:T(8,128)(2,1)} convert(f32[18992,1536]{1,0:T(8,128)} %scatter_custom_fusion) | non-fusion elementwise | flops 29171712 | bytes 175030272 | tf_op jit(solution)/shard_map/convert_element_type | solution.py:124
  (114 shorter events, 1.3 us)
Async XLA Ops:
  7.2 926.2 %all-gather.9.cloned.1.call-start = ((), (), s32[]{:S(2)}) async-start(), calls=%async_computation.7 | async-start | bytes 5308416 | tf_op jit(solution)/shard_map/all_gather | solution.py:118
  7.9 1144.3 %reduce-scatter.6.cloned.1.call-start = ((), (), s32[]{:S(2)}) async-start(), calls=%async_computation.5 | async-start | bytes 56623104 | tf_op jit(solution)/shard_map/reduce_scatter | solution.py:110
  605.6 0.9 copy-start.27
  605.6 1.1 copy-start.28
  605.6 1.4 copy-start.29
  605.6 1.6 copy-start.30
  605.6 298.9 %copy-start.23 = (bf16[192,256]{1,0:T(8,128)(2,1)S(1)}, bf16[192,256]{1,0:T(8,128)(2,1)}, u32[]{:S(2)}) copy-start(bf16[192,256]{1,0:T(8,128)(2,1)} %param.17) | copy-start | bytes 294916
  605.7 312.8 %copy-start.24 = (bf16[192,256]{1,0:T(8,128)(2,1)S(1)}, bf16[192,256]{1,0:T(8,128)(2,1)}, u32[]{:S(2)}) copy-start(bf16[192,256]{1,0:T(8,128)(2,1)} %param.19) | copy-start | bytes 294916
  605.7 581.3 %all-gather.7.cloned.1.call-start = ((), (), s32[]{:S(2)}) async-start(), calls=%async_computation.6 | async-start | bytes 5308416 | tf_op jit(solution)/shard_map/all_gather | solution.py:112
  606.4 1563.9 %all-gather.11.cloned.1.call-start = ((), (), s32[]{:S(2)}) async-start(), calls=%async_computation.12 | async-start | bytes 113246208 | tf_op jit(solution)/shard_map/all_gather | solution.py:120
  901.8 326.6 %copy-start.19 = (f32[1536]{0:T(1024)}, f32[1536]{0:T(1024)S(1)}, u32[]{:S(2)}) copy-start(f32[1536]{0:T(1024)S(1)} %convert_element_type.97) | copy-start | bytes 18436
  918.5 237.8 %copy-start.9 = (bf16[1536,256]{1,0:T(8,128)(2,1)}, bf16[1536,256]{1,0:T(8,128)(2,1)S(1)}, u32[]{:S(2)}) copy-start(bf16[1536,256]{1,0:T(8,128)(2,1)S(1)} %all_gather.41) | copy-start | bytes 2359300
  1156.3 72.1 %copy-start.21 = (f32[2,1024]{1,0:T(2,128)}, f32[2,1024]{1,0:T(2,128)S(1)}, u32[]{:S(2)}) copy-start(f32[2,1024]{1,0:T(2,128)S(1)} %add_rsqrt_fusion) | copy-start | bytes 24580
  1160.7 1.3 copy-start.5
  1203.2 25.2 slice-start.3
  1215.9 12.5 slice-start.4
  1233.4 37.6 %copy-start = (f32[1024,128]{0,1:T(8,128)S(1)}, f32[1024,128]{0,1:T(8,128)}, u32[]{:S(2)}) copy-start(f32[1024,128]{0,1:T(8,128)} %get-tuple-element.34) | copy-start | bytes 1572868
  1233.4 37.6 %copy-start.3 = (f32[1024,128]{0,1:T(8,128)S(1)}, f32[1024,128]{0,1:T(8,128)}, u32[]{:S(2)}) copy-start(f32[1024,128]{0,1:T(8,128)} %get-tuple-element.35) | copy-start | bytes 1572868
  1233.4 37.6 %copy-start.6 = (f32[2,1024,256]{1,2,0:T(8,128)S(1)}, f32[2,1024,256]{1,2,0:T(8,128)}, u32[]{:S(2)}) copy-start(f32[2,1024,256]{1,2,0:T(8,128)} %copy-done.5) | copy-start | bytes 6291460
  1274.1 13.1 copy-start.15
  1274.1 13.1 copy-start.16
  1333.4 36.8 %copy-start.4 = (f32[1024,128]{0,1:T(8,128)S(1)}, f32[1024,128]{0,1:T(8,128)}, u32[]{:S(2)}) copy-start(f32[1024,128]{0,1:T(8,128)} %get-tuple-element.35) | copy-start | bytes 1572868
  1370.2 125.9 %copy-start.17 = (bf16[2,1024,2,128,1]{1,3,4,2,0:T(8,128)(2,1)S(1)}, bf16[2,1024,2,128,1]{1,3,4,2,0:T(8,128)(2,1)}, u32[]{:S(2)}) copy-start(bf16[2,1024,2,128,1]{1,3,4,2,0:T(8,128)(2,1)} %fusion.78) | copy-start | bytes 3145732
  1496.0 125.9 %copy-start.1 = (f32[1024,128]{0,1:T(8,128)S(1)}, f32[1024,128]{0,1:T(8,128)}, u32[]{:S(2)}) copy-start(f32[1024,128]{0,1:T(8,128)} %get-tuple-element.34) | copy-start | bytes 1572868
  1496.0 129.3 %copy-start.10 = (bf16[1536,256]{1,0:T(8,128)(2,1)S(1)}, bf16[1536,256]{1,0:T(8,128)(2,1)}, u32[]{:S(2)}) copy-start(bf16[1536,256]{1,0:T(8,128)(2,1)} %copy-done.9) | copy-start | bytes 2359300
  1624.4 1.0 copy-start.7
  1643.9 31.3 %slice-start = ((s8[12582912]{0:T(1024)(128)(4,1)}), s8[4194304]{0:T(1024)(128)(4,1)S(1)}, s32[]{:S(2)}) async-start(s8[12582912]{0:T(1024)(128)(4,1)} %bitcast.211), calls=%async_computation.13 | async-start | bytes 8388608
  1656.3 19.0 slice-start.1
  1656.3 19.0 slice-start.2
  1675.3 26.4 %slice-start.5 = ((s8[6291456]{0:T(1024)(128)(4,1)}), s8[2097152]{0:T(1024)(128)(4,1)S(1)}, s32[]{:S(2)}) async-start(s8[6291456]{0:T(1024)(128)(4,1)} %bitcast.218), calls=%async_computation.18 | async-start | bytes 4194304
  1685.1 16.6 slice-start.6
  1685.1 16.6 copy-start.11
  1685.1 16.6 copy-start.20
  1685.1 16.6 copy-start.22
  1729.5 1.2 copy-start.14
  1729.5 8.0 copy-start.8
  1729.6 878.7 %reduce-scatter.12.cloned.1.call-start = ((), (), s32[]{:S(2)}) async-start(), calls=%async_computation.10 | async-start | bytes 1769472 | tf_op jit(solution)/shard_map/reduce_scatter | solution.py:123
  1737.1 6.9 copy-start.13
  1737.1 871.2 %reduce-scatter.10.cloned.1.call-start = ((), (), s32[]{:S(2)}) async-start(), calls=%async_computation.9 | async-start | bytes 1769472 | tf_op jit(solution)/shard_map/reduce_scatter | solution.py:123
  1743.9 864.4 %reduce-scatter.14.cloned.1.call-start = ((), (), s32[]{:S(2)}) async-start(), calls=%async_computation.11 | async-start | bytes 10616832 | tf_op jit(solution)/shard_map/reduce_scatter | solution.py:123
  1794.3 814.0 %reduce-scatter.8.cloned.1.call-start = ((), (), s32[]{:S(2)}) async-start(), calls=%async_computation.8 | async-start | bytes 10616832 | tf_op jit(solution)/shard_map/reduce_scatter | solution.py:123
  1794.5 17.1 copy-start.18
  1794.6 24.3 copy-start.2
  1818.9 9.2 copy-start.12
  1818.9 9.4 copy-start.25
  1818.9 9.4 copy-start.26
Sparse Core Ops, SparseCore 0:
  9.8 35.9 all-gather.8
  605.8 546.3 reduce-scatter.5
  1154.0 32.9 all-gather.6
  1729.7 440.5 all-gather.10
  2174.0 29.8 reduce-scatter.11
  2207.5 29.8 reduce-scatter.9
  2241.4 67.4 reduce-scatter.13
  2312.8 67.4 reduce-scatter.7
where the time goes:
time: 2640 us; the launch traced here: 2620 us
  other arithmetic  597 us (23%)
  local copies, waits for them, and re-layouts  578 us (22%)
  matrix products  545 us (21%)
  waiting for transfers between devices  520 us (20%)
  blocking collectives  359 us (14%)
    gather x1, local copies, waits for them, and re-layouts, device_step(): looked = jnp.take(table_part, jnp.where(is_owned, local_idx, 0), axis=0)  549 us
    scatter-add x3, other arithmetic, device_step(): jax.ops.segment_sum(all_dx.reshape(-1, model_width), seg_idx.reshape(-1),...  390 us
    unnamed x2, blocking collectives  318 us
    all_gather x1, waiting for transfers between devices, device_step(): all_dx = lax.all_gather(d_x, 'fsdp')  300 us
    reduce_scatter x1, waiting for transfers between devices, device_step(): x_rows = lax.psum_scatter(looked, 'fsdp', scatter_dimension=0)  195 us
    dot_general x1, matrix products, block_fwd_bwd(): jnp.einsum('bkgqs,bqkgd->bskd', d_scores, q_rot, preferred_element_type=j...  126 us
    dot_general x1, matrix products, block_fwd_bwd(): jnp.einsum('bkgqs,bskd->bqkgd', d_scores, k_rot, preferred_element_type=j...  124 us
    convert_element_type x1, other arithmetic, device_step(): return (block_out, grad_part.astype(jnp.bfloat16)) + reduced  55.4 us
  transfers between devices with their start and end apart: 8, of which 3 were waited for; matrix products, arithmetic and copies ran while one was open for 45% of the time, Pallas kernels for 0%

commit v1 on v0

v1 whole, which is shorter than its diff:
```python
import functools

import jax
import jax.numpy as jnp
from jax import lax
from jax.experimental import pallas as pl
from jax.experimental.pallas import tpu as pltpu
from jax.sharding import PartitionSpec as P

F32 = jnp.float32
BF16 = jnp.bfloat16
I32 = jnp.int32
MESH = pl.DeviceIdType.MESH

LANE = 128
SUB = 8
HEAD_DIM = LANE
ROPE_THETA = 1.0e6
NORM_EPS = 1e-6
MASK_VALUE = -1e30

N_DEV = 8
SEQ = 1024
SEQS = 2
TOK = SEQ * SEQS
D = 1536
HEADS = 12
KV = 2
GROUP = HEADS // KV
ROWS = 18992
HOT = 4096
CAP = 176
COLD = N_DEV * CAP
BUF = HOT + COLD
QKV = D + 2 * KV * HEAD_DIM
VMEM_MAX = 66_000_000


def params(**kw):
    return pltpu.CompilerParams(vmem_limit_bytes=VMEM_MAX, **kw)


ANY = pl.BlockSpec(memory_space=pl.ANY)


def full(*shape):
    return pl.BlockSpec(shape, lambda *i: (0,) * len(shape))


def by_row(*shape):
    return pl.BlockSpec(shape, lambda i, *_: (i,) + (0,) * (len(shape) - 1))


def shape_of(dtype, *shape):
    return jax.ShapeDtypeStruct(shape, dtype)


def row_sum(v):
    return jnp.sum(v, axis=-1, keepdims=True)


def row_mean(v):
    return jnp.mean(v, axis=-1, keepdims=True)


def col_sum(v):
    return jnp.sum(v, axis=0, keepdims=True)


def iota(dtype, shape, dim):
    return lax.broadcasted_iota(I32, shape, dim).astype(dtype)


def cost(flops, nbytes):
    return pl.CostEstimate(flops=int(flops), bytes_accessed=int(nbytes), transcendentals=0)


def dot(a, b, dims):
    return lax.dot_general(a, b, (dims, ((), ())), preferred_element_type=F32)


NN = ((1,), (0,))
NT = ((1,), (1,))
TN = ((0,), (0,))


def index_kernel(me_ref, mine_ref, ids_ref, xi_ref, own_ref, ovf_ref, rank_ref):
    me = me_ref[0]
    r_io = lax.broadcasted_iota(I32, (LANE, LANE), 0)
    c_io = lax.broadcasted_iota(I32, (LANE, LANE), 1)
    own_s = lax.broadcasted_iota(I32, (8, 1), 0)
    lo_s = jnp.maximum(own_s * ROWS, HOT).astype(F32)
    hi_s = (own_s * ROWS + ROWS).astype(F32)
    up = (r_io < c_io).astype(BF16)
    run = jnp.zeros((8, 1), F32)
    for b in range(TOK // LANE):
        blk = mine_ref[:, b * LANE : (b + 1) * LANE]
        hit = jnp.logical_and(blk >= lo_s, blk < hi_s)
        one = hit.astype(F32)
        rank = dot(one.astype(BF16), up, NN) + run
        run = run + row_sum(one)
        slot = jnp.minimum(rank, CAP - 1) + own_s.astype(F32) * CAP + HOT
        pick = col_sum(jnp.where(hit, slot, 0.0))
        xi_ref[b : b + 1, :] = jnp.where(blk < HOT, blk, pick).astype(I32)
    lane = lax.broadcasted_iota(I32, (1, 64), 1)
    own_l = lax.rem(lane, 8)
    lo_l = jnp.maximum(own_l * ROWS, HOT).astype(F32)
    hi_l = (own_l * ROWS + ROWS).astype(F32)
    low = (r_io > c_io).astype(BF16)
    run = jnp.zeros((1, 64), F32)
    for b in range(TOK // LANE):
        blk = ids_ref[b * LANE : (b + 1) * LANE, :]
        hit = jnp.logical_and(blk >= lo_l, blk < hi_l)
        one = hit.astype(F32)
        rank = dot(low, one.astype(BF16), NN) + run
        run = run + col_sum(one)
        rank_ref[b * LANE : (b + 1) * LANE, :] = jnp.where(hit, rank, -1.0)
    ovf_ref[...] = jnp.broadcast_to(jnp.max(run, axis=1, keepdims=True), ovf_ref.shape)
    slot_io = lax.broadcasted_iota(I32, (1, 256), 1).astype(F32)
    first = (me * ROWS).astype(F32)
    for s in range(N_DEV):
        col = lane == s * 8 + me
        acc = jnp.zeros((8, 256), F32)
        for b in range(TOK // 256):
            rk = rank_ref[b * 256 : (b + 1) * 256, :]
            idb = ids_ref[b * 256 : (b + 1) * 256, :]
            rk1 = row_sum(jnp.where(col, rk, 0.0))
            loc = row_sum(jnp.where(col, idb, 0.0)) - first + 1.0
            hitv = jnp.where(rk1 == slot_io, loc, 0.0)
            acc = acc + jnp.sum(hitv.reshape(32, 8, 256), axis=0)
        own_ref[s : s + 1, :] = col_sum(acc).astype(I32) - 1


def index_maps(me, mine, ids64):
    return pl.pallas_call(
        index_kernel,
        grid_spec=pltpu.PrefetchScalarGridSpec(
            num_scalar_prefetch=1,
            grid=(1,),
            in_specs=[full(1, TOK), full(TOK, 64)],
            out_specs=[
                full(TOK // LANE, LANE),
                full(8, 256),
                full(8, LANE),
            ],
            scratch_shapes=[pltpu.VMEM((TOK, 64), F32)],
        ),
        out_shape=[
            shape_of(I32, TOK // LANE, LANE),
            shape_of(I32, 8, 256),
            shape_of(F32, 8, LANE),
        ],
        compiler_params=params(),
        cost_estimate=cost(5e9, 2e6),
        name="index_maps",
    )(me, mine, ids64)


def merge_kernel(row_ref, col_ref, tgt_ref, rep_ref):
    n = row_ref.shape[1]
    for b in range(n // LANE):
        row = row_ref[:, b * LANE : (b + 1) * LANE]
        pair = jnp.floor(row * 0.5)
        best = jnp.full((8, LANE), float(n), F32)
        for c in range(n // LANE):
            other = jnp.floor(col_ref[c * LANE : (c + 1) * LANE, :] * 0.5)
            kk = (lax.broadcasted_iota(I32, (LANE, 1), 0) + c * LANE).astype(F32)
            hit = jnp.where(other == pair, kk, float(n))
            best = jnp.minimum(best, jnp.min(hit.reshape(16, 8, LANE), axis=0))
        rep = jnp.min(best, axis=0, keepdims=True)
        par = row - 2.0 * pair
        tgt_ref[b : b + 1, :] = (2.0 * rep + par).astype(I32)
        rep_ref[b : b + 1, :] = rep.astype(I32)


def merge_maps(row, col):
    n = row.shape[1]
    return pl.pallas_call(
        merge_kernel,
        out_shape=[shape_of(I32, n // LANE, LANE)] * 2,
        compiler_params=params(),
        cost_estimate=cost(5e9, 1e6),
        name="merge_maps",
    )(row, col)


def gather_kernel(n, idx_s, idx_ref, src_ref, out_ref, buf, sem):
    i = pl.program_id(0)

    def fetch(blk, slot):
        def body(q, c):
            for u in range(8):
                j = q * 8 + u
                r = lax.shift_right_logical(jnp.maximum(idx_s[blk, j], 0), 1)
                pltpu.make_async_copy(
                    src_ref.at[pl.ds(pl.multiple_of(r * 2, 2), 2), :],
                    buf.at[slot, pl.ds(pl.multiple_of(j * 2, 2), 2), :],
                    sem.at[slot],
                ).start()
            return c

        lax.fori_loop(0, n // 8, body, 0)

    slot = lax.rem(i, 2)

    @pl.when(i == 0)
    def _():
        fetch(0, 0)

    @pl.when(i + 1 < pl.num_programs(0))
    def _():
        fetch(i + 1, 1 - slot)

    idx = jnp.maximum(idx_ref[pl.ds(i, 1), :][:, :n], 0)
    k_io = lax.broadcasted_iota(I32, (2 * n, n), 0)
    j_io = lax.broadcasted_iota(I32, (2 * n, n), 1)
    want = 2 * j_io + jnp.bitwise_and(idx, 1)
    pick = (k_io == want).astype(BF16)
    pltpu.make_async_copy(src_ref.at[pl.ds(0, 2 * n), :], buf.at[slot], sem.at[slot]).wait()
    out_ref[0] = dot(pick, buf[slot], TN).astype(BF16)


def gather_rows(src, idx, n):
    blocks = idx.shape[0]
    return pl.pallas_call(
        functools.partial(gather_kernel, n),
        grid_spec=pltpu.PrefetchScalarGridSpec(
            num_scalar_prefetch=1,
            grid=(blocks,),
            in_specs=[full(*idx.shape), ANY],
            out_specs=by_row(1, n, D),
            scratch_shapes=[pltpu.VMEM((2, 2 * n, D), BF16), pltpu.SemaphoreType.DMA((2,))],
        ),
        out_shape=shape_of(BF16, blocks, n, D),
        compiler_params=params(),
        cost_estimate=cost(2e10, blocks * n * D * 6),
        name="gather_rows",
    )(idx, idx, src)


CHUNKS = 8
HALF = HOT // 2
CH = HALF // CHUNKS


def lookup_kernel(table, send, buf, stage, ld_sem, st_sem, a_send, a_recv, b_send, b_recv, d_send, d_recv, c_send, c_recv):
    me = lax.axis_index("fsdp")
    barrier = pltpu.get_barrier_semaphore()
    for off in range(1, N_DEV):
        pl.semaphore_signal(barrier, inc=1, device_id=(lax.rem(me + off, N_DEV),), device_id_type=MESH)
    pl.semaphore_wait(barrier, N_DEV - 1)

    def a_rows(k):
        return pl.ds(k * CH, CH)

    def b_rows(k):
        return pl.ds(HALF + k * CH, CH)

    def remote(src, rows, s_sem, r_sem, dev):
        return pltpu.make_async_remote_copy(src_ref=src.at[rows, :], dst_ref=buf.at[rows, :], send_sem=s_sem, recv_sem=r_sem, device_id=(dev,), device_id_type=MESH)

    def cold(off):
        dst = lax.rem(me + off, N_DEV)
        return pltpu.make_async_remote_copy(
            src_ref=send.at[dst],
            dst_ref=buf.at[pl.ds(pl.multiple_of(HOT + me * CAP, 16), CAP), :],
            send_sem=c_send.at[off],
            recv_sem=c_recv.at[off],
            device_id=(dst,),
            device_id_type=MESH,
        )

    def cold_in(off):
        src = lax.rem(me - off + N_DEV, N_DEV)
        return pltpu.make_async_remote_copy(
            src_ref=send.at[0],
            dst_ref=buf.at[pl.ds(pl.multiple_of(HOT + src * CAP, 16), CAP), :],
            send_sem=c_send.at[off],
            recv_sem=c_recv.at[off],
            device_id=(src,),
            device_id_type=MESH,
        )

    root = me == 0
    nxt = {2: 6, 6: 4, 1: 5, 5: 7, 7: 3}
    for k in range(CHUNKS):

        @pl.when(root)
        def _(k=k):
            remote(table, a_rows(k), a_send.at[k], a_recv.at[k], 2).start()
            remote(table, b_rows(k), b_send.at[k], b_recv.at[k], 1).start()
            remote(table, a_rows(k), d_send.at[k], d_recv.at[k], 1).start()

        for dev in (2, 6, 4):

            @pl.when(me == dev)
            def _(k=k, dev=dev):
                remote(table, a_rows(k), a_send.at[k], a_recv.at[k], 0).wait_recv()
                if dev in nxt:
                    remote(buf, a_rows(k), a_send.at[k], a_recv.at[k], nxt[dev]).start()
                remote(buf, a_rows(k), d_send.at[k], d_recv.at[k], dev + 1).start()

        for dev in (1, 5, 7, 3):

            @pl.when(me == dev)
            def _(k=k, dev=dev):
                remote(table, b_rows(k), b_send.at[k], b_recv.at[k], 0).wait_recv()
                if dev in nxt:
                    remote(buf, b_rows(k), b_send.at[k], b_recv.at[k], nxt[dev]).start()
                if dev != 1:
                    remote(buf, b_rows(k), d_send.at[k], d_recv.at[k], dev - 1).start()

        if 1 <= k + 1 < N_DEV:
            cold(k + 1).start()

    ld = pltpu.make_async_copy(send.at[me], stage.at[pl.ds(0, CAP), :], ld_sem)
    ld.start()
    ld.wait()
    st = pltpu.make_async_copy(stage.at[pl.ds(0, CAP), :], buf.at[pl.ds(pl.multiple_of(HOT + me * CAP, 16), CAP), :], st_sem)
    st.start()
    st.wait()

    @pl.when(root)
    def _():
        big = pltpu.make_async_copy(table.at[pl.ds(0, HOT), :], stage, ld_sem)
        big.start()
        big.wait()
        out = pltpu.make_async_copy(stage, buf.at[pl.ds(0, HOT), :], st_sem)
        out.start()
        out.wait()

    for k in range(CHUNKS):
        for dev in (1, 3, 5, 7):

            @pl.when(me == dev)
            def _(k=k):
                remote(table, a_rows(k), d_send.at[k], d_recv.at[k], 0).wait_recv()

        for dev in (2, 4, 6):

            @pl.when(me == dev)
            def _(k=k):
                remote(table, b_rows(k), d_send.at[k], d_recv.at[k], 0).wait_recv()

    for off in range(1, N_DEV):
        cold_in(off).wait_recv()
    for off in range(1, N_DEV):
        cold(off).wait_send()
    for k in range(CHUNKS):

        @pl.when(root)
        def _(k=k):
            remote(table, a_rows(k), a_send.at[k], a_recv.at[k], 2).wait_send()
            remote(table, b_rows(k), b_send.at[k], b_recv.at[k], 1).wait_send()
            remote(table, a_rows(k), d_send.at[k], d_recv.at[k], 1).wait_send()

        for dev in (2, 6, 4):

            @pl.when(me == dev)
            def _(k=k, dev=dev):
                if dev in nxt:
                    remote(buf, a_rows(k), a_send.at[k], a_recv.at[k], nxt[dev]).wait_send()
                remote(buf, a_rows(k), d_send.at[k], d_recv.at[k], dev + 1).wait_send()

        for dev in (1, 5, 7, 3):

            @pl.when(me == dev)
            def _(k=k, dev=dev):
                if dev in nxt:
                    remote(buf, b_rows(k), b_send.at[k], b_recv.at[k], nxt[dev]).wait_send()
                if dev != 1:
                    remote(buf, b_rows(k), d_send.at[k], d_recv.at[k], dev - 1).wait_send()


def lookup_exchange(table, send):
    dma = pltpu.SemaphoreType.DMA
    return pl.pallas_call(
        lookup_kernel,
        in_specs=[ANY] * 2,
        out_specs=ANY,
        out_shape=shape_of(BF16, BUF, D),
        scratch_shapes=[pltpu.VMEM((HOT, D), BF16), dma, dma] + [dma((CHUNKS,))] * 6 + [dma((N_DEV,))] * 2,
        compiler_params=params(collective_id=0, has_side_effects=True),
        cost_estimate=cost(8e10, 4e7),
        name="lookup_exchange",
    )(table, send)


def proj_kernel(x_ref, gain_ref, w_ref, bias_ref, cos_ref, sin_ref, hid_ref, qkv_ref):
    x = x_ref[...].astype(F32)
    inv = lax.rsqrt(row_mean(x * x) + NORM_EPS)
    hid = (x * inv * gain_ref[...]).astype(BF16)
    hid_ref[...] = hid
    cos_t = cos_ref[...]
    sin_t = sin_ref[...]
    for c in range(0, QKV, 512):
        lin = dot(hid, w_ref[:, c : c + 512], NN) + bias_ref[:, c : c + 512]
        for h in range(0, 512, HEAD_DIM):
            v = lin[:, h : h + HEAD_DIM]
            if c + h < D + KV * HEAD_DIM:
                v = v * cos_t + pltpu.roll(v, HEAD_DIM // 2, 1) * sin_t
            qkv_ref[:, c + h : c + h + HEAD_DIM] = v.astype(BF16)


def proj(x, gain, w, bias, cos_t, sin_t):
    tm = 256
    per = SEQ // tm
    return pl.pallas_call(
        proj_kernel,
        grid=(TOK // tm,),
        in_specs=[
            by_row(tm, D),
            full(1, D),
            full(D, QKV),
            full(1, QKV),
            pl.BlockSpec((tm, HEAD_DIM), lambda i: (lax.rem(i, per), 0)),
            pl.BlockSpec((tm, HEAD_DIM), lambda i: (lax.rem(i, per), 0)),
        ],
        out_specs=[by_row(tm, D), by_row(tm, QKV)],
        out_shape=[shape_of(BF16, TOK, D), shape_of(BF16, TOK, QKV)],
        compiler_params=params(),
        cost_estimate=cost(2 * TOK * D * QKV, 3e7),
        name="proj",
    )(x, gain, w, bias, cos_t, sin_t)


QB = 256
LOG2E = 1.4426950408889634


def rot_back(g, cos_t, sin_t):
    return g * cos_t - pltpu.roll(g, HEAD_DIM // 2, 1) * sin_t


def col_sums(g):
    return jnp.sum(g.reshape(g.shape[0] // 8, 8, g.shape[1]), axis=0)


def attn_kernel(q_ref, k_ref, v_ref, do_ref, cos_ref, sin_ref, o_ref, dq_ref, dk_ref, dv_ref, bq_ref, bk_ref, bv_ref, dk_acc, dv_acc):
    g = pl.program_id(2)
    scale = HEAD_DIM**-0.5

    @pl.when(g == 0)
    def _():
        dk_acc[...] = jnp.zeros_like(dk_acc)
        dv_acc[...] = jnp.zeros_like(dv_acc)

    bq = jnp.zeros((8, HEAD_DIM), F32)
    diag = lax.broadcasted_iota(I32, (QB, QB), 0) >= lax.broadcasted_iota(I32, (QB, QB), 1)
    for b in range(SEQ // QB):
        rows = slice(b * QB, (b + 1) * QB)
        n = (b + 1) * QB
        q = q_ref[rows, :]
        k = k_ref[:n, :]
        v = v_ref[:n, :]
        do = do_ref[rows, :]
        t = dot(q, k, NT) * (scale * LOG2E)
        last = jnp.where(diag, t[:, n - QB :], MASK_VALUE)
        t = last if b == 0 else jnp.concatenate([t[:, : n - QB], last], axis=1)
        e = jnp.exp2(t - jnp.max(t, axis=-1, keepdims=True))
        p = e * (1.0 / row_sum(e))
        pb = p.astype(BF16)
        o_ref[rows, :] = dot(pb, v, NN).astype(BF16)
        dp = dot(do, v, NT)
        delta = row_sum(dp * p)
        ds = (p * ((dp - delta) * scale)).astype(BF16)
        dq = rot_back(dot(ds, k, NN), cos_ref[rows, :], sin_ref[rows, :])
        bq = bq + col_sums(dq)
        dq_ref[rows, :] = dq.astype(BF16)
        dk_acc[:n, :] += dot(ds, q, TN)
        dv_acc[:n, :] += dot(pb, do, TN)
    bq_ref[0] = bq

    @pl.when(g == GROUP - 1)
    def _():
        dk = rot_back(dk_acc[...], cos_ref[...], sin_ref[...])
        dv = dv_acc[...]
        dk_ref[...] = dk.astype(BF16)
        dv_ref[...] = dv.astype(BF16)
        bk_ref[0] = col_sums(dk)
        bv_ref[0] = col_sums(dv)


def attention(qkv, d_attn, cos_t, sin_t):
    head = lambda b, h, g: (b, h * GROUP + g)
    kv = lambda b, h, g: (b, h)
    full = lambda b, h, g: (0, 0)
    blk = (SEQ, HEAD_DIM)
    return pl.pallas_call(
        attn_kernel,
        grid=(SEQS, KV, GROUP),
        in_specs=[
            pl.BlockSpec(blk, head),
            pl.BlockSpec(blk, lambda b, h, g: (b, HEADS + h)),
            pl.BlockSpec(blk, lambda b, h, g: (b, HEADS + KV + h)),
            pl.BlockSpec(blk, head),
            pl.BlockSpec(blk, full),
            pl.BlockSpec(blk, full),
        ],
        out_specs=[
            pl.BlockSpec(blk, head),
            pl.BlockSpec(blk, head),
            pl.BlockSpec(blk, kv),
            pl.BlockSpec(blk, kv),
            pl.BlockSpec((1, 8, HEAD_DIM), lambda b, h, g: (b, 0, h * GROUP + g)),
            pl.BlockSpec((1, 8, HEAD_DIM), lambda b, h, g: (b, 0, h)),
            pl.BlockSpec((1, 8, HEAD_DIM), lambda b, h, g: (b, 0, h)),
        ],
        out_shape=[
            shape_of(BF16, TOK, D),
            shape_of(BF16, TOK, D),
            shape_of(BF16, TOK, KV * HEAD_DIM),
            shape_of(BF16, TOK, KV * HEAD_DIM),
            shape_of(F32, SEQS, 8, D),
            shape_of(F32, SEQS, 8, KV * HEAD_DIM),
            shape_of(F32, SEQS, 8, KV * HEAD_DIM),
        ],
        scratch_shapes=[pltpu.VMEM((SEQ, HEAD_DIM), F32)] * 2,
        compiler_params=params(),
        cost_estimate=cost(6 * 2 * TOK * SEQ * D, 3e7),
        name="attention",
    )(qkv, qkv, qkv, d_attn, cos_t, sin_t)


def dx_kernel(dq_ref, dk_ref, dv_ref, w_ref, x_ref, go_ref, gain_ref, dx_ref, gg_ref, gg_acc):
    i = pl.program_id(0)

    @pl.when(i == 0)
    def _():
        gg_acc[...] = jnp.zeros_like(gg_acc)

    kvw = KV * HEAD_DIM
    dh = dot(dq_ref[...], w_ref[:, :D], NT)
    dh = dh + dot(dk_ref[...], w_ref[:, D : D + kvw], NT)
    dh = dh + dot(dv_ref[...], w_ref[:, D + kvw :], NT)
    x = x_ref[...].astype(F32)
    inv = lax.rsqrt(row_mean(x * x) + NORM_EPS)
    xn = x * inv
    gg_acc[...] += col_sums(dh * xn)
    dn = dh * gain_ref[...]
    mean = row_mean(dn * xn)
    dx_ref[...] = go_ref[...].astype(F32) + inv * (dn - xn * mean)
    gg_ref[...] = gg_acc[...]


def input_grad(dq, dk, dv, w, x, go, gain):
    tm = 256
    tok = lambda n: by_row(tm, n)
    return pl.pallas_call(
        dx_kernel,
        grid=(TOK // tm,),
        in_specs=[
            tok(D),
            tok(KV * HEAD_DIM),
            tok(KV * HEAD_DIM),
            full(D, QKV),
            tok(D),
            tok(D),
            full(1, D),
        ],
        out_specs=[tok(D), full(8, D)],
        out_shape=[shape_of(F32, TOK, D), shape_of(F32, 8, D)],
        scratch_shapes=[pltpu.VMEM((8, D), F32)],
        compiler_params=params(),
        cost_estimate=cost(2 * TOK * D * QKV, 4e7),
        name="input_grad",
    )(dq, dk, dv, w, x, go, gain)


def wgrad_kernel(h_ref, dq_ref, dk_ref, dv_ref, o_ref):
    h = h_ref[...]
    kvw = KV * HEAD_DIM
    o_ref[:, :D] = dot(h, dq_ref[...], TN)
    o_ref[:, D : D + kvw] = dot(h, dk_ref[...], TN)
    o_ref[:, D + kvw :] = dot(h, dv_ref[...], TN)


def qkv_weight_grad(hid, dq, dk, dv):
    tn = 256
    const = lambda n: full(TOK, n)
    return pl.pallas_call(
        wgrad_kernel,
        grid=(D // tn,),
        in_specs=[pl.BlockSpec((TOK, tn), lambda i: (0, i)), const(D), const(KV * HEAD_DIM), const(KV * HEAD_DIM)],
        out_specs=by_row(tn, QKV),
        out_shape=shape_of(F32, D, QKV),
        compiler_params=params(),
        cost_estimate=cost(2 * TOK * D * QKV, 3e7),
        name="qkv_weight_grad",
    )(hid, dq, dk, dv)


def scatter_kernel(xi_s, dx_ref, hot_ref, cold_ref, acc, sem):
    i = pl.program_id(0)
    tm = dx_ref.shape[0]

    @pl.when(i == 0)
    def _():
        def zero(b, c):
            acc[pl.ds(pl.multiple_of(b * LANE, LANE), LANE), :] = jnp.zeros((LANE, D), F32)
            return c

        lax.fori_loop(0, BUF // LANE, zero, 0)

    def body(q, c):
        for u in range(8):
            t = q * 8 + u
            r = xi_s[i * (tm // LANE) + lax.shift_right_logical(t, 7), jnp.bitwise_and(t, 127)]
            acc[pl.ds(r, 1), :] += dx_ref[pl.ds(t, 1), :]
        return c

    lax.fori_loop(0, tm // 8, body, 0)

    @pl.when(i == pl.num_programs(0) - 1)
    def _():
        a = pltpu.make_async_copy(acc.at[pl.ds(0, HOT), :], hot_ref, sem.at[0])
        b = pltpu.make_async_copy(acc.at[pl.ds(HOT, COLD), :], cold_ref, sem.at[1])
        a.start()
        b.start()
        a.wait()
        b.wait()


def scatter_rows(xi, dx):
    tm = 256
    return pl.pallas_call(
        scatter_kernel,
        grid_spec=pltpu.PrefetchScalarGridSpec(
            num_scalar_prefetch=1,
            grid=(TOK // tm,),
            in_specs=[by_row(tm, D)],
            out_specs=[ANY] * 2,
            scratch_shapes=[pltpu.VMEM((BUF, D), F32), pltpu.SemaphoreType.DMA((2,))],
        ),
        out_shape=[shape_of(F32, HOT, D), shape_of(F32, COLD, D)],
        compiler_params=params(),
        cost_estimate=cost(3e10, 5e7),
        name="scatter_rows",
    )(xi, dx)


ZROWS = 512


def final_kernel(me_s, own_s, tgt_s, rep_s, hot_ref, cold_ref, out_ref, zero, cold, acc, stage, hot, z_sem, c_sem, h_sem, p_sem):
    me = me_s[0]
    pltpu.make_async_copy(cold_ref, cold, c_sem).start()
    zero[...] = jnp.zeros_like(zero)

    def fill(lo, n):
        return pltpu.make_async_copy(zero.at[pl.ds(0, n), :], out_ref.at[pl.ds(lo, n), :], z_sem)

    spans = []
    lo = HOT
    while lo < ROWS:
        n = min(ZROWS, ROWS - lo)
        spans.append((lo, n))
        lo += n
    for lo, n in spans:
        fill(lo, n).start()

    @pl.when(me == 0)
    def _():
        pltpu.make_async_copy(hot_ref, hot, h_sem).start()

    @pl.when(me != 0)
    def _():
        for lo in range(0, HOT, ZROWS):
            fill(lo, ZROWS).start()

    def clear(b, c):
        acc[pl.ds(pl.multiple_of(b * LANE, LANE), LANE), :] = jnp.zeros((LANE, D), F32)
        return c

    lax.fori_loop(0, 2 * COLD // LANE, clear, 0)

    @pl.when(me == 0)
    def _():
        pltpu.make_async_copy(hot_ref, hot, h_sem).wait()
        pltpu.make_async_copy(hot, out_ref.at[pl.ds(0, HOT), :], h_sem).start()

    pltpu.make_async_copy(cold_ref, cold, c_sem).wait()

    def add(q, c):
        for u in range(8):
            j = q * 8 + u
            r = tgt_s[lax.shift_right_logical(j, 7), jnp.bitwise_and(j, 127)]
            acc[pl.ds(r, 1), :] += cold[pl.ds(j, 1), :]
        return c

    lax.fori_loop(0, COLD // 8, add, 0)

    def conv(b, c):
        rows = pl.ds(pl.multiple_of(b * LANE, LANE), LANE)
        stage[rows, :] = acc[rows, :].astype(BF16)
        return c

    lax.fori_loop(0, 2 * COLD // LANE, conv, 0)

    for lo, n in spans:
        fill(lo, n).wait()

    @pl.when(me == 0)
    def _():
        pltpu.make_async_copy(hot, out_ref.at[pl.ds(0, HOT), :], h_sem).wait()

    @pl.when(me != 0)
    def _():
        for lo in range(0, HOT, ZROWS):
            fill(lo, ZROWS).wait()

    def pair_copy(j, row):
        return pltpu.make_async_copy(
            stage.at[pl.ds(pl.multiple_of(j * 2, 2), 2), :], out_ref.at[pl.ds(pl.multiple_of(row, 2), 2), :], p_sem
        )

    def put(j, count):
        rep = rep_s[lax.shift_right_logical(j, 7), jnp.bitwise_and(j, 127)]
        s = lax.div(j, CAP)
        row = own_s[s, j - s * CAP]
        go = jnp.logical_and(rep == j, row >= 0)

        @pl.when(go)
        def _():
            pair_copy(j, lax.shift_right_logical(jnp.maximum(row, 0), 1) * 2).start()

        return count + go.astype(I32)

    count = lax.fori_loop(0, COLD, put, jnp.int32(0))

    def drain(j, c):
        pair_copy(0, 0).wait()
        return c

    lax.fori_loop(0, count, drain, 0)


def final_rows(me, own, tgt, rep, hot, cold):
    dma = pltpu.SemaphoreType.DMA
    return pl.pallas_call(
        final_kernel,
        grid_spec=pltpu.PrefetchScalarGridSpec(
            num_scalar_prefetch=4,
            grid=(1,),
            in_specs=[ANY] * 2,
            out_specs=ANY,
            scratch_shapes=[
                pltpu.VMEM((ZROWS, D), BF16),
                pltpu.VMEM((COLD, D), F32),
                pltpu.VMEM((2 * COLD, D), F32),
                pltpu.VMEM((2 * COLD, D), BF16),
                pltpu.VMEM((HOT, D), BF16),
                dma,
                dma,
                dma,
                dma,
            ],
        ),
        out_shape=shape_of(BF16, ROWS, D),
        compiler_params=params(),
        cost_estimate=cost(4e10, 8e7),
        name="final_rows",
    )(me, own, tgt, rep, hot, cold)


def swap_kernel(same, x_ref, out_ref, own_sem, send_sem, recv_sem):
    me = lax.axis_index("fsdp")
    barrier = pltpu.get_barrier_semaphore()
    for off in range(1, N_DEV):
        pl.semaphore_signal(barrier, inc=1, device_id=(lax.rem(me + off, N_DEV),), device_id_type=MESH)
    pl.semaphore_wait(barrier, N_DEV - 1)

    def copy(off):
        dst = lax.rem(me + off, N_DEV)
        return pltpu.make_async_remote_copy(
            src_ref=x_ref.at[0 if same else dst],
            dst_ref=out_ref.at[me],
            send_sem=send_sem.at[off],
            recv_sem=recv_sem.at[off],
            device_id=(dst,),
            device_id_type=MESH,
        )

    def inward(off):
        src = lax.rem(me - off + N_DEV, N_DEV)
        return pltpu.make_async_remote_copy(
            src_ref=x_ref.at[0],
            dst_ref=out_ref.at[src],
            send_sem=send_sem.at[off],
            recv_sem=recv_sem.at[off],
            device_id=(src,),
            device_id_type=MESH,
        )

    for off in range(1, N_DEV):
        copy(off).start()
    own = pltpu.make_async_copy(x_ref.at[0 if same else me], out_ref.at[me], own_sem)
    own.start()
    own.wait()
    for off in range(1, N_DEV):
        inward(off).wait_recv()
    for off in range(1, N_DEV):
        copy(off).wait_send()


def swap_blocks(x, cid):
    dma = pltpu.SemaphoreType.DMA
    return pl.pallas_call(
        functools.partial(swap_kernel, x.shape[0] == 1),
        in_specs=[ANY],
        out_specs=ANY,
        out_shape=jax.ShapeDtypeStruct((N_DEV,) + x.shape[1:], x.dtype),
        scratch_shapes=[dma, dma((N_DEV,)), dma((N_DEV,))],
        compiler_params=params(collective_id=cid, has_side_effects=True),
        name="swap_blocks",
    )(x)


SLOW = LANE


def general_lookup(table, ids, first):
    def step(c, x):
        loc = lax.dynamic_slice(ids, (0, c * SLOW), (N_DEV, SLOW)) - first
        owned = (loc >= 0) & (loc < ROWS)
        rows = jnp.take(table, jnp.where(owned, loc, 0), axis=0)
        rows = jnp.where(owned[..., None], rows, jnp.zeros((), BF16))
        got = swap_blocks(rows, 1).astype(F32).sum(0).astype(BF16)
        return lax.dynamic_update_slice(x, got, (c * SLOW, 0))

    return lax.fori_loop(0, TOK // SLOW, step, jnp.zeros((TOK, D), BF16))


def general_scatter(d_x, ids, first):
    def step(c, acc):
        loc = lax.dynamic_slice(ids, (0, c * SLOW), (N_DEV, SLOW)) - first
        owned = (loc >= 0) & (loc < ROWS)
        got = swap_blocks(lax.dynamic_slice(d_x, (c * SLOW, 0), (SLOW, D))[None], 2)
        seg = jnp.where(owned, loc, ROWS)
        return acc.at[seg.reshape(-1)].add(got.reshape(-1, D), mode="drop")

    acc = lax.fori_loop(0, TOK // SLOW, step, jnp.zeros((ROWS, D), F32))
    return acc.astype(BF16)


def rope_tables():
    half = HEAD_DIM // 2
    inv_freq = jnp.power(ROPE_THETA, -(jnp.arange(half, dtype=F32) * 2.0 / HEAD_DIM))
    angles = jnp.arange(SEQ, dtype=F32)[:, None] * inv_freq[None, :]
    cos_h, sin_h = jnp.cos(angles), jnp.sin(angles)
    return jnp.concatenate([cos_h, cos_h], axis=-1), jnp.concatenate([-sin_h, sin_h], axis=-1)


def device_step(tok_ids, grad_out, table, gain_p, wq_p, bq_p, wk_p, bk_p, wv_p, bv_p, wo_p):
    ax = "fsdp"
    me = lax.axis_index(ax)
    me1 = me.reshape(1).astype(I32)
    first = me * ROWS
    kvw = KV * HEAD_DIM
    mine = tok_ids.reshape(1, TOK).astype(F32)
    small = jnp.concatenate([mine[0]] + [v.astype(F32) for v in (gain_p, bq_p, bk_p, bv_p)])
    small = lax.all_gather(small, ax)
    w_qkv = lax.all_gather(jnp.concatenate([wq_p, wk_p, wv_p], axis=1), ax, axis=0, tiled=True)
    w_out = lax.all_gather(wo_p, ax, axis=0, tiled=True)
    ids_f = small[:, :TOK]
    cuts = [TOK, TOK + D // N_DEV, TOK + 2 * (D // N_DEV), TOK + 2 * (D // N_DEV) + kvw // N_DEV, TOK + 2 * (D // N_DEV) + 2 * (kvw // N_DEV)]
    gain, b_q, b_k, b_v = (small[:, a:b].reshape(1, -1) for a, b in zip(cuts[:-1], cuts[1:], strict=True))
    bias = jnp.concatenate([b_q, b_k, b_v], axis=1)
    cos_t, sin_t = rope_tables()

    xi, own, most = index_maps(me1, mine, jnp.repeat(ids_f.T, N_DEV, axis=1))
    over = most[0, 0] > CAP
    send = gather_rows(table, own, CAP)
    buf = lookup_exchange(table, send)
    x = lax.cond(
        over,
        lambda: general_lookup(table, ids_f.astype(I32), first).reshape(TOK, D),
        lambda: gather_rows(buf, xi, LANE).reshape(TOK, D),
    )
    x = lax.optimization_barrier(x)
    go = grad_out.reshape(TOK, D)

    hid, qkv = proj(x, gain, w_qkv, bias, cos_t, sin_t)
    d_attn = dot(go, w_out, NT).astype(BF16)
    attn, dq, dk, dv, s_q, s_k, s_v = attention(qkv, d_attn, cos_t, sin_t)
    block_out = (x.astype(F32) + dot(attn, w_out, NN)).astype(BF16).reshape(grad_out.shape)
    g_out = lax.psum_scatter(dot(attn, go, TN), ax, scatter_dimension=0, tiled=True)
    d_x, s_g = input_grad(dq, dk, dv, w_qkv, x, go, gain)
    g_qkv = lax.psum_scatter(qkv_weight_grad(hid, dq, dk, dv), ax, scatter_dimension=0, tiled=True)

    parts = [s_g.sum(0), s_q.sum((0, 1)), s_k.sum((0, 1)), s_v.sum((0, 1))]
    vec = jnp.concatenate([p.reshape(N_DEV, -1) for p in parts], axis=1)
    vec = lax.all_to_all(vec, ax, 0, 0, tiled=True).sum(0)

    hot, cold = scatter_rows(xi, d_x)
    cold = lax.all_to_all(cold.reshape(N_DEV, CAP, D), ax, 0, 0, tiled=True).reshape(COLD, D)
    hot = lax.psum_scatter(hot, ax, scatter_dimension=0, tiled=True).astype(BF16)
    hot = lax.all_gather(hot, ax, axis=0, tiled=True)
    flat = own[:, :CAP].reshape(1, COLD).astype(F32)
    tgt, rep = merge_maps(flat, flat.reshape(COLD, 1))
    grad_table = lax.cond(
        over,
        lambda: general_scatter(d_x, ids_f.astype(I32), first),
        lambda: final_rows(me1, own, tgt, rep, hot, cold),
    )

    e0, e1, e2 = D // N_DEV, 2 * (D // N_DEV), 2 * (D // N_DEV) + kvw // N_DEV
    return (
        block_out,
        grad_table,
        vec[:e0],
        g_qkv[:, :D],
        vec[e0:e1],
        g_qkv[:, D : D + kvw],
        vec[e1:e2],
        g_qkv[:, D + kvw :],
        vec[e2:],
        g_out,
    )


def solution(mesh):
    row = P("fsdp", None)
    vec = P("fsdp")
    act = P("fsdp", None, None)
    weights = (vec, row, vec, row, vec, row, vec, row)
    return jax.shard_map(
        device_step, mesh=mesh, in_specs=(row, act, row) + weights, out_specs=(act, row) + weights, check_vma=False
    )
```

time: 2640 us -> 1010 us (0.38)
  other arithmetic: 597 us -> 10.2 us
  local copies, waits for them, and re-layouts: 578 us -> 19.6 us
  Pallas kernels: 0 us -> 506 us
  matrix products: 545 us -> 46.7 us
  blocking collectives: 359 us -> 6.03 us
  waiting for transfers between devices: 520 us -> 385 us
    gather x1 -> x0, local copies, waits for them, and re-layouts: 549 us -> none  [device_step(): looked = jnp.take(table_part, jnp.where(is_owned, local_idx, 0), axis=0)]
    pallas_call x0 -> x11, Pallas kernels: none -> 506 us  [the longest x1 170 us: lookup_exchange(): pl.pallas_call(lookup_kernel, in_specs=[ANY] * 2, out_specs=ANY, out_shap...]
    dot_general x17 -> x3, matrix products: 499 us -> 46.7 us  [dot(): return lax.dot_general(a, b, (dims, ((), ())), preferred_element_type=F32)]
    scatter-add x3 -> x0, other arithmetic: 390 us -> none  [device_step(): jax.ops.segment_sum(all_dx.reshape(-1, model_width), seg_idx.reshape(-1),...]
    unnamed x2 -> x0, blocking collectives: 318 us -> none
    all_gather x3, waiting for transfers between devices: 324 us -> 63.7 us  [the longest x1 63.7 us: device_step(): hot = lax.all_gather(hot, ax, axis=0, tiled=True)]
    convert_element_type x9 -> x2, other arithmetic: 99.7 us -> 3.21 us  [the longest x1 3.21 us: device_step(): lax.psum_scatter(hot, ax, scatter_dimension=0, tiled=True).astype(BF16)]
    reduce_scatter x5 -> x3, waiting for transfers between devices: 195 us -> 283 us  [the longest x1 158 us: device_step(): lax.psum_scatter(hot, ax, scatter_dimension=0, tiled=True).astype(BF16)]
  transfers between devices with their start and end apart: 8 -> 8, of which waited for: 3 -> 5; matrix products, arithmetic and copies ran while one was open for 45% -> 7% of each run, Pallas kernels for 0% -> 32%
where the time goes in v1:
time: 1010 us; the launch traced here: 1000 us
  Pallas kernels  506 us (50%)
  waiting for transfers between devices  385 us (38%)
  matrix products  46.7 us (5%)
  local copies, waits for them, and re-layouts  19.6 us (2%)
  between operations  15.4 us (2%)
  other arithmetic  10.2 us (1%)
    pallas_call x1, Pallas kernels, lookup_exchange(): pl.pallas_call(lookup_kernel, in_specs=[ANY] * 2, out_specs=ANY, out_shap...  170 us
    reduce_scatter x1, waiting for transfers between devices, device_step(): lax.psum_scatter(hot, ax, scatter_dimension=0, tiled=True).astype(BF16)  158 us
    reduce_scatter x1, waiting for transfers between devices, device_step(): lax.psum_scatter(qkv_weight_grad(hid, dq, dk, dv), ax, scatter_dimension=...  121 us
    pallas_call x1, Pallas kernels, attention(): pl.pallas_call(attn_kernel, grid=(SEQS, KV, GROUP), in_specs=[pl.BlockSpe...  111 us
    pallas_call x1, Pallas kernels, final_rows(): pl.pallas_call(final_kernel, grid_spec=pltpu.PrefetchScalarGridSpec(num_s...  67 us
    all_gather x1, waiting for transfers between devices, device_step(): hot = lax.all_gather(hot, ax, axis=0, tiled=True)  63.7 us
    pallas_call x2, Pallas kernels, gather_rows(): pl.pallas_call(functools.partial(gather_kernel, n), grid_spec=pltpu.Prefe...  54.6 us
    dot_general x3, matrix products, dot(): return lax.dot_general(a, b, (dims, ((), ())), preferred_element_type=F32)  46.7 us
  transfers between devices with their start and end apart: 8, of which 5 were waited for; matrix products, arithmetic and copies ran while one was open for 7% of the time, Pallas kernels for 32%

profile of v1, /device:TPU:0, one launch (start us, length us, event | category | flops | bytes accessed | tf_op | source)
XLA Modules:
  0.0 1003.1 jit_solution(5774048294350244175)
XLA Ops:
  7.2 0.0 all-reduce.3.cloned.1.call-start
  7.2 0.7 convert_bitcast_fusion
  7.9 2.7 concatenate.18
  10.7 0.3 dynamic-update-slice
  11.0 0.6 copy-done.2
  11.7 0.0 all-gather.7.cloned.1.call-start
  11.7 0.7 all-gather.7.cloned.1.call-update
  12.4 0.0 all-gather.5.cloned.1.call-start
  12.5 2.2 pad_maximum_fusion
  14.7 0.0 reduce-scatter.4.cloned.1.call-start
  14.7 0.6 copy.26
  15.3 2.0 fusion.2
  17.3 1.3 pad_maximum_fusion.1
  18.7 38.1 %all-reduce.3.cloned.1.call-done = f32[19968]{0:T(1024)} async-done(((f32[19968]{0:T(1024)}), f32[19968]{0:T(1024)}) %all-reduce.3.cloned.1.call-update) | async-done | bytes 79888
  56.8 1.0 reshape.198
  57.8 1.3 copy.24.ids_ref
  59.1 6.1 index_maps.1
  65.2 0.6 copy-done.8
  65.8 26.8 %gather_rows.3.send = bf16[8,176,1536]{2,1,0:T(8,128)(2,1)} custom-call(s32[8,256]{1,0:T(8,128)S(1)} %get-tuple-element.305.idx_s.idx_ref, s32[8,256]{1,0:T(8,128)S(1)} %get-tuple-element.305.idx_s.idx_ref, bf16[18992,1536]{1,0:T(8,128)(2,1)} %table.1), custom_call_target="tpu_custom_call" | custom-call | flops 20000000000 | bytes 12976128 | tf_op jit(solution)/shard_map/gather_rows/pallas_call | solution.py:225
  92.5 0.1 fusion.5
  92.6 0.6 reshape.172
  93.3 0.6 reshape.173
  93.9 0.1 fusion.4
  94.0 0.7 reshape.171
  94.6 0.7 reshape.170.gain_ref
  95.3 1.2 slice.43
  97.2 169.7 %lookup_exchange.1 = bf16[5504,1536]{1,0:T(8,128)(2,1)} custom-call(bf16[18992,1536]{1,0:T(8,128)(2,1)} %table.1, bf16[8,176,1536]{2,1,0:T(8,128)(2,1)} %gather_rows.3.send), custom_call_target="tpu_custom_call" | custom-call | flops 80000000000 | bytes 40000000 | tf_op jit(solution)/shard_map/lookup_exchange/pallas_call | solution.py:377
  266.9 37.6 %conditional.2 = (bf16[2048,1536]{1,0:T(8,128)(2,1)}) conditional(s32[]{:T(128)} %bitcast.11, (s32[16,128]{1,0:T(8,128)S(1)}, bf16[5504,1536]{1,0:T(8,128)(2,1)}) %tuple.56, (f32[8,2048]{1,0:T(8,128)S(1)}, s32[]{:T(128)}, bf16[18992,1536]{1,0:T(8,128)(2,1)}) %tuple.57), branch_computations={%region_0.0_spmd, %region_1.5_spmd} | conditional | flops 20000000000 | bytes 23352586 | solution.py:875
  266.9 27.8 %gather_rows.2 = bf16[16,128,1536]{2,1,0:T(8,128)(2,1)} custom-call(s32[16,128]{1,0:T(8,128)S(1)} %get-tuple-element.247.idx_s.idx_ref, s32[16,128]{1,0:T(8,128)S(1)} %get-tuple-element.247.idx_s.idx_ref, bf16[5504,1536]{1,0:T(8,128)(2,1)} %get-tuple-element.248.src_ref), custom_call_target="tpu_custom_call" | custom-call | flops 20000000000 | bytes 18874368 | tf_op jit(solution)/shard_map/cond/branch_0_fun/gather_rows/pallas_call | solution.py:225
  304.5 0.6 pad_maximum_fusion.4.bias_ref
  305.1 15.1 %convolution_convert_fusion.do_ref = bf16[2048,1536]{1,0:T(8,128)(2,1)} fusion(bf16[2048,1536]{1,0:T(8,128)(2,1)} %bitcast.53, bf16[1536,1536]{1,0:T(8,128)(2,1)} %all-gather.7.cloned.1.call-done), kind=kOutput, calls=%fused_computation.14 | convolution fusion | flops 9666822144 | bytes 17301504 | tf_op jit(solution)/shard_map/dot_general | solution.py:79
  320.2 20.9 %proj.1 = (bf16[2048,1536]{1,0:T(8,128)(2,1)}, bf16[2048,2048]{1,0:T(8,128)(2,1)}) custom-call(bf16[2048,1536]{1,0:T(8,128)(2,1)} %get-tuple-element.485.x_ref, f32[1,1536]{1,0:T(1,128)} %reshape.170.gain_ref, bf16[1536,2048]{1,0:T(8,128)(2,1)} %all-gather.5.cloned.1.call-done.w_ref, f32[1,2048]{1,0:T(1,128)} %pad_maximum_fusion.4.bias_ref, ...), custom_call_target="tpu_custom_call" | custom-call | flops 12884901888 | bytes 30000000 | tf_op jit(solution)/shard_map/proj/pallas_call | solution.py:408
  341.1 110.8 %attention.1 = (bf16[2048,1536]{1,0:T(8,128)(2,1)}, bf16[2048,1536]{1,0:T(8,128)(2,1)}, bf16[2048,256]{1,0:T(8,128)(2,1)}, bf16[2048,256]{1,0:T(8,128)(2,1)}, f3...) custom-call(bf16[2048,2048]{1,0:T(8,128)(2,1)} %get-tuple-element.306.q_ref.k_ref.v_ref, ...), custom_call_target="tpu_custom_call" | custom-call | flops 38654705664 | bytes 30000000 | tf_op jit(solution)/shard_map/attention/pallas_call | solution.py:489
  451.9 23.8 %input_grad.1 = (f32[2048,1536]{1,0:T(8,128)}, f32[8,1536]{1,0:T(8,128)}) custom-call(bf16[2048,1536]{1,0:T(8,128)(2,1)} %get-tuple-element.308.dq_ref, bf16[2048,256]{1,0:T(8,128)(2,1)} %get-tuple-element.309.dk_ref, bf16[2048,256]{1,0:T(8,128)(2,1)} %get-tuple-element.310.dv_ref, bf16[1536,2048]{1,0:T(8,128)(2,1)} %all-gather.5.cloned.1.call-done.w_ref, ...), custom_call_target="tpu_custom_call" | custom-call | flops 12884901888 | bytes 40000000 | tf_op jit(solution)/shard_map/input_grad/pallas_call | solution.py:549
  475.7 30.3 %scatter_rows.1 = (f32[4096,1536]{1,0:T(8,128)}, f32[1408,1536]{1,0:T(8,128)}) custom-call(s32[16,128]{1,0:T(8,128)S(1)} %get-tuple-element.304.xi_s, f32[2048,1536]{1,0:T(8,128)} %get-tuple-element.311.dx_ref), custom_call_target="tpu_custom_call" | custom-call | flops 30000001024 | bytes 50000000 | tf_op jit(solution)/shard_map/scatter_rows/pallas_call | solution.py:626
  506.0 0.0 reduce-scatter.4.cloned.1.call-update
  506.1 0.2 reduce-scatter.6.cloned.1.call-start
  506.3 19.3 %qkv_weight_grad.1 = f32[1536,2048]{1,0:T(8,128)} custom-call(bf16[2048,1536]{1,0:T(8,128)(2,1)} %get-tuple-element.320.h_ref, bf16[2048,1536]{1,0:T(8,128)(2,1)} %get-tuple-element.308.dq_ref, bf16[2048,256]{1,0:T(8,128)(2,1)} %get-tuple-element.309.dk_ref, bf16[2048,256]{1,0:T(8,128)(2,1)} %get-tuple-element.310.dv_ref), custom_call_target="tpu_custom_call" | custom-call | flops 12884901888 | bytes 30000000 | tf_op jit(solution)/shard_map/qkv_weight_grad/pallas_call | solution.py:581
  525.6 0.0 all-gather.9.cloned.1.call-start
  525.6 157.9 %reduce-scatter.4.cloned.1.call-done = f32[512,1536]{1,0:T(8,128)} async-done(((f32[4096,1536]{1,0:T(8,128)}), f32[512,1536]{1,0:T(8,128)}) %reduce-scatter.4.cloned.1.call-update) | async-done | bytes 3145744 | tf_op jit(solution)/shard_map/reduce_scatter | solution.py:897
  683.5 3.2 convert_element_type.75
  686.7 0.0 reduce-scatter.8.cloned.1.call-start
  686.8 15.6 %fusion.9 = f32[1536,1536]{1,0:T(8,128)} fusion(bf16[2048,1536]{1,0:T(8,128)(2,1)} %get-tuple-element.307, bf16[2048,1536]{1,0:T(8,128)(2,1)} %bitcast.55), kind=kOutput, calls=%fused_computation.37 | convolution fusion | flops 9663676416 | bytes 22020096 | tf_op jit(solution)/shard_map/dot_general | solution.py:79
  702.5 0.8 copy-done.3
  703.4 0.1 reshape.178
  703.5 0.1 reshape.180
  703.6 0.1 reshape.179
  703.7 0.1 reshape.177
  703.7 0.1 pad_maximum_fusion.3
  703.8 6.0 all_to_all.14
  709.9 3.9 all-to-all-start
  713.7 0.7 convert_element_type.73.row_ref
  714.4 1.1 convert_element_type.77.col_ref
  715.6 3.3 merge_maps.1
  718.8 16.0 %add_convert_fusion = bf16[2048,1536]{1,0:T(8,128)(2,1)} fusion(bf16[2048,1536]{1,0:T(8,128)(2,1)} %get-tuple-element.485.x_ref, bf16[2048,1536]{1,0:T(8,128)(2,1)} %get-tuple-element.307, bf16[1536,1536]{1,0:T(8,128)(2,1)} %all-gather.7.cloned.1.call-done), kind=kOutput, calls=%fused_computation.13 | convolution fusion | flops 9673113600 | bytes 23592960 | tf_op jit(solution)/shard_map/dot_general | solution.py:79
  734.8 0.6 fusion.7
  735.4 0.6 fusion.8
  736.1 120.6 %reduce-scatter.6.cloned.1.call-done = f32[192,2048]{1,0:T(8,128)} async-done(((f32[1536,2048]{1,0:T(8,128)}), f32[192,2048]{1,0:T(8,128)}) %reduce-scatter.6.cloned.1.call-update) | async-done | bytes 1572880 | tf_op jit(solution)/shard_map/reduce_scatter | solution.py:889
  856.6 2.4 slice.63
  859.0 1.8 fusion.3
  860.8 63.7 %all-gather.9.cloned.1.call-done = bf16[4096,1536]{1,0:T(8,128)(2,1)} async-done(((bf16[512,1536]{1,0:T(8,128)(2,1)}), bf16[4096,1536]{1,0:T(8,128)(2,1)}) %all-gather.9.cloned.1.call-update) | async-done | bytes 12582928 | tf_op jit(solution)/shard_map/all_gather | solution.py:898
  924.5 67.0 %conditional.3 = (bf16[18992,1536]{1,0:T(8,128)(2,1)}) conditional(s32[]{:T(128)} %bitcast.11, (f32[8,176,1536]{2,1,0:T(8,128)}, s32[1]{0:T(128)}, s32[8,256]{1,0:T(8,128)S(1)}, s32[11,128]{1,0:T(8,128)S(1)}, s32[11,128]{1,0:T(8,128)S(1)}, /*index=5*/bf16[4096,1536]{1,0:T(8,128)(2,1)}) %tuple.115, (f32[8,2048]{1,0:T(8,128)S(1)}, s32[]{:T(128)}, ...), branch_computations={%region_6.7_spmd, %region_7.11_spmd} | conditional | flops 40000000000 | bytes 312316128 | solution.py:901
  924.5 67.0 %final_rows.1 = bf16[18992,1536]{1,0:T(8,128)(2,1)} custom-call(s32[1]{0:T(128)} %get-tuple-element.259.me_s, s32[8,256]{1,0:T(8,128)S(1)} %get-tuple-element.260.own_s, s32[11,128]{1,0:T(8,128)S(1)} %get-tuple-element.261.tgt_s, s32[11,128]{1,0:T(8,128)S(1)} %get-tuple-element.262.rep_s, bf16[4096,1536]{1,0:T(8,128)(2,1)} %get-tuple-element.263.hot_ref, ...), custom_call_target="tpu_custom_call" | custom-call | flops 40000000000 | bytes 80000000 | tf_op jit(solution)/shard_map/cond/branch_0_fun/final_rows/pallas_call | solution.py:740
  991.5 4.4 reduce-scatter.8.cloned.1.call-done
  (41 shorter events, 0.3 us)
Async XLA Ops:
  7.2 49.6 %all-reduce.3.cloned.1.call-start = ((), (), s32[]{:S(2)}) async-start(), calls=%async_computation.11 | async-start | bytes 163840
  11.0 0.6 copy-start.2
  11.7 293.4 %all-gather.7.cloned.1.call-start = ((), (), s32[]{:S(2)}) async-start(), calls=%async_computation.6 | async-start | bytes 5308416 | tf_op jit(solution)/shard_map/all_gather | solution.py:864
  12.4 307.8 %all-gather.5.cloned.1.call-start = ((), (), s32[]{:S(2)}) async-start(), calls=%async_computation.5 | async-start | bytes 7077888 | tf_op jit(solution)/shard_map/all_gather | solution.py:863
  14.7 668.8 %reduce-scatter.4.cloned.1.call-start = ((), (), s32[]{:S(2)}) async-start(), calls=%async_computation.7 | async-start | bytes 28311552 | tf_op jit(solution)/shard_map/reduce_scatter | solution.py:897
  57.7 209.1 %copy-start = (f32[8,2048]{1,0:T(8,128)}, f32[8,2048]{1,0:T(8,128)S(1)}, u32[]{:S(2)}) copy-start(f32[8,2048]{1,0:T(8,128)S(1)} %get-tuple-element.349) | copy-start | bytes 196612
  65.2 0.6 copy-start.8
  266.9 37.6 %copy-start.5 = (f32[1,1536]{1,0:T(1,128)S(1)}, f32[1,1536]{1,0:T(1,128)}, u32[]{:S(2)}) copy-start(f32[1,1536]{1,0:T(1,128)} %reshape.171) | copy-start | bytes 18436
  266.9 37.6 %copy-start.10 = (f32[1,256]{1,0:T(1,128)S(1)}, f32[1,256]{1,0:T(1,128)}, u32[]{:S(2)}) copy-start(f32[1,256]{1,0:T(1,128)} %reshape.172) | copy-start | bytes 3076
  266.9 37.6 %copy-start.11 = (f32[1,256]{1,0:T(1,128)S(1)}, f32[1,256]{1,0:T(1,128)}, u32[]{:S(2)}) copy-start(f32[1,256]{1,0:T(1,128)} %reshape.173) | copy-start | bytes 3076
  506.1 350.6 %reduce-scatter.6.cloned.1.call-start = ((), (), s32[]{:S(2)}) async-start(), calls=%async_computation.9 | async-start | bytes 14155776 | tf_op jit(solution)/shard_map/reduce_scatter | solution.py:889
  525.6 398.9 %all-gather.9.cloned.1.call-start = ((), (), s32[]{:S(2)}) async-start(), calls=%async_computation.8 | async-start | bytes 14155776 | tf_op jit(solution)/shard_map/all_gather | solution.py:898
  686.7 309.2 %reduce-scatter.8.cloned.1.call-start = ((), (), s32[]{:S(2)}) async-start(), calls=%async_computation.10 | async-start | bytes 10616832 | tf_op jit(solution)/shard_map/reduce_scatter | solution.py:887
  702.4 0.9 copy-start.3
  702.4 1.0 copy-start.7
  702.4 1.0 copy-start.6
  702.4 1.2 copy-start.4
  709.9 3.9 copy-start.9
  709.9 150.9 %all-to-all-start = ((f32[8,176,1536]{2,1,0:T(8,128)}), f32[8,176,1536]{2,1,0:T(8,128)}, u32[]{:S(2)}, u32[]{:S(2)}) async-start(f32[8,176,1536]{2,1,0:T(8,128)} %bitcast.48), calls=%async_computation | async-start | bytes 17301504 | tf_op jit(solution)/shard_map/all_to_all | solution.py:896
  718.8 205.6 %copy-start.1 = (f32[8,2048]{1,0:T(8,128)S(1)}, f32[8,2048]{1,0:T(8,128)}, u32[]{:S(2)}) copy-start(f32[8,2048]{1,0:T(8,128)} %copy-done) | copy-start | bytes 196612
Sparse Core Ops, SparseCore 0:
  11.8 44.9 all-reduce.2
  58.6 32.2 all-gather.6
  93.3 60.0 all-gather.4
  506.2 177.2 reduce-scatter.3
  686.8 169.7 reduce-scatter.5
  858.9 65.5 all-gather.8
  928.5 67.4 reduce-scatter.7

commit v2 on v1

--- a/solution.py
+++ b/solution.py
@@ -20,6 +20,7 @@
 MASK_VALUE = -1e30
 
 N_DEV = 8
+OTHERS = range(1, N_DEV)
 SEQ = 1024
 SEQS = 2
 TOK = SEQ * SEQS
@@ -67,6 +68,14 @@
     return jnp.sum(v, axis=0, keepdims=True)
 
 
+def loop(n, body):
+    def step(k, c):
+        body(k)
+        return c
+
+    lax.fori_loop(0, n, step, 0)
+
+
 def iota(dtype, shape, dim):
     return lax.broadcasted_iota(I32, shape, dim).astype(dtype)
 
@@ -84,76 +93,218 @@
 TN = ((0,), (0,))
 
 
-def index_kernel(me_ref, mine_ref, ids_ref, xi_ref, own_ref, ovf_ref, rank_ref):
-    me = me_ref[0]
-    r_io = lax.broadcasted_iota(I32, (LANE, LANE), 0)
-    c_io = lax.broadcasted_iota(I32, (LANE, LANE), 1)
-    own_s = lax.broadcasted_iota(I32, (8, 1), 0)
+HALF = HOT // 2
+CHUNKS = 16
+PACK = 20
+
+
+def meet(me):
+    barrier = pltpu.get_barrier_semaphore()
+    for off in OTHERS:
+        pl.semaphore_signal(barrier, inc=1, device_id=(lax.rem(me + off, N_DEV),), device_id_type=MESH)
+    pl.semaphore_wait(barrier, N_DEV - 1)
+
+
+def push(src, dst, s_sem, r_sem, dev):
+    return pltpu.make_async_remote_copy(
+        src_ref=src, dst_ref=dst, send_sem=s_sem, recv_sem=r_sem, device_id=(dev,), device_id_type=MESH
+    )
+
+
+def rows_of(ref, start, n, align=SUB):
+    return ref.at[pl.ds(pl.multiple_of(start, align), n), :]
+
+
+def prologue_kernel(pk_ref, table, hot, all_ref, xi_ref, hid_ref, cold_ref, own_ref, most_ref, got, code, own_f, stage, ld_sem, p_send, p_recv, c_send, c_recv, d_send, d_recv):
+    me = lax.axis_index("fsdp")
+    n = HALF // CHUNKS
+    got[me] = pk_ref[...]
+    meet(me)
+
+    def pack_to(off):
+        return push(pk_ref, got.at[me], p_send.at[off], p_recv.at[off], lax.rem(me + off, N_DEV))
+
+    def pack_from(off):
+        src = lax.rem(me - off + N_DEV, N_DEV)
+        return push(pk_ref, got.at[src], p_send.at[off], p_recv.at[off], src)
+
+    for off in OTHERS:
+        pack_to(off).start()
+
+    def part(ref, half, k):
+        return rows_of(ref, half * HALF + k * n, n)
+
+    def chain(src, half, k, dev):
+        return push(part(src, half, k), part(hot, half, k), c_send.at[k], c_recv.at[k], dev)
+
+    def pass_on(src, half, k, dev):
+        return push(part(src, half, k), part(hot, half, k), d_send.at[k], d_recv.at[k], dev)
+
+    def root_copy():
+        return pltpu.make_async_copy(rows_of(table, 0, HOT), stage, ld_sem)
+
+    def root_store():
+        return pltpu.make_async_copy(stage, hot, ld_sem)
+
+    nxt = {2: 6, 6: 4, 1: 5, 5: 7, 7: 3}
+
+    @pl.when(me == 0)
+    def _():
+        def go(k):
+            chain(table, 0, k, 2).start()
+            pass_on(table, 1, k, 1).start()
+
+        loop(CHUNKS, go)
+        root_copy().start()
+
+    r_io = iota(I32, (LANE, LANE), 0)
+    c_io = iota(I32, (LANE, LANE), 1)
+    own_s = iota(I32, (N_DEV, 1), 0)
     lo_s = jnp.maximum(own_s * ROWS, HOT).astype(F32)
     hi_s = (own_s * ROWS + ROWS).astype(F32)
     up = (r_io < c_io).astype(BF16)
-    run = jnp.zeros((8, 1), F32)
+    run = jnp.zeros((N_DEV, 1), F32)
     for b in range(TOK // LANE):
-        blk = mine_ref[:, b * LANE : (b + 1) * LANE]
+        blk = pk_ref[b : b + 1, :]
         hit = jnp.logical_and(blk >= lo_s, blk < hi_s)
         one = hit.astype(F32)
         rank = dot(one.astype(BF16), up, NN) + run
         run = run + row_sum(one)
-        slot = jnp.minimum(rank, CAP - 1) + own_s.astype(F32) * CAP + HOT
-        pick = col_sum(jnp.where(hit, slot, 0.0))
-        xi_ref[b : b + 1, :] = jnp.where(blk < HOT, blk, pick).astype(I32)
-    lane = lax.broadcasted_iota(I32, (1, 64), 1)
-    own_l = lax.rem(lane, 8)
-    lo_l = jnp.maximum(own_l * ROWS, HOT).astype(F32)
-    hi_l = (own_l * ROWS + ROWS).astype(F32)
-    low = (r_io > c_io).astype(BF16)
-    run = jnp.zeros((1, 64), F32)
-    for b in range(TOK // LANE):
-        blk = ids_ref[b * LANE : (b + 1) * LANE, :]
-        hit = jnp.logical_and(blk >= lo_l, blk < hi_l)
-        one = hit.astype(F32)
-        rank = dot(low, one.astype(BF16), NN) + run
-        run = run + col_sum(one)
-        rank_ref[b * LANE : (b + 1) * LANE, :] = jnp.where(hit, rank, -1.0)
-    ovf_ref[...] = jnp.broadcast_to(jnp.max(run, axis=1, keepdims=True), ovf_ref.shape)
-    slot_io = lax.broadcasted_iota(I32, (1, 256), 1).astype(F32)
+        slot = jnp.minimum(rank, CAP - 1) + own_s.astype(F32) * CAP
+        slot = col_sum(jnp.where(hit, slot, 0.0))
+        is_hot = blk < HOT
+        xi_ref[b : b + 1, :] = jnp.where(is_hot, blk, slot + HOT).astype(I32)
+        hid_ref[b : b + 1, :] = jnp.where(is_hot, blk, -1.0).astype(I32)
+        cold_ref[b : b + 1, :] = jnp.where(is_hot, -1.0, slot).astype(I32)
+
+    for off in OTHERS:
+        pack_from(off).wait_recv()
+    all_ref[...] = got[...]
+    per = TOK // LANE
+    grid = jnp.concatenate([got[s][:per, :] for s in range(N_DEV)], axis=0)
+    same = (lax.div(r_io[: N_DEV * per, : N_DEV * per], per) == lax.div(c_io[: N_DEV * per, : N_DEV * per], per)).astype(F32)
+    tot = jnp.zeros((1, N_DEV * per), F32)
+    flat = grid.T
+    for o in range(N_DEV):
+        hit = jnp.logical_and(flat >= max(o * ROWS, HOT), flat < (o + 1) * ROWS)
+        cnt = jnp.broadcast_to(col_sum(hit.astype(F32)), (SUB, N_DEV * per))
+        tot = jnp.maximum(tot, dot(cnt.astype(BF16), same.astype(BF16), NN)[:1, :])
+    most_ref[...] = jnp.broadcast_to(jnp.max(tot, axis=-1, keepdims=True), most_ref.shape)
     first = (me * ROWS).astype(F32)
-    for s in range(N_DEV):
-        col = lane == s * 8 + me
-        acc = jnp.zeros((8, 256), F32)
-        for b in range(TOK // 256):
-            rk = rank_ref[b * 256 : (b + 1) * 256, :]
-            idb = ids_ref[b * 256 : (b + 1) * 256, :]
-            rk1 = row_sum(jnp.where(col, rk, 0.0))
-            loc = row_sum(jnp.where(col, idb, 0.0)) - first + 1.0
-            hitv = jnp.where(rk1 == slot_io, loc, 0.0)
-            acc = acc + jnp.sum(hitv.reshape(32, 8, 256), axis=0)
-        own_ref[s : s + 1, :] = col_sum(acc).astype(I32) - 1
-
-
-def index_maps(me, mine, ids64):
+    hit = jnp.logical_and(flat >= jnp.maximum(me * ROWS, HOT).astype(F32), flat < first + ROWS)
+    one = hit.astype(F32)
+    rank = dot((r_io > c_io).astype(BF16), one.astype(BF16), NN)
+    before = jnp.where(r_io < c_io, 1.0, 0.0)[: N_DEV * per, : N_DEV * per] * same
+    cnt = jnp.broadcast_to(col_sum(one), (SUB, N_DEV * per))
+    rank = rank + dot(cnt.astype(BF16), before.astype(BF16), NN)[:1, :]
+    code[...] = jnp.where(hit, rank * CODE + (flat - first), -1.0)
+    own_f[...] = jnp.zeros_like(own_f)
+    slots = iota(F32, (1, 2 * LANE), 1)
+    lane = iota(I32, (1, N_DEV * per), 1)
+
+    def listing(c):
+        val = row_sum(jnp.where(lane == c, code[...], 0.0))
+        rk = jnp.floor(val * (1.0 / CODE))
+        loc = val - rk * CODE + 1.0
+        add = col_sum(jnp.where(rk == slots, loc, 0.0))
+        s = lax.div(c, per)
+        own_f[pl.ds(s, 1), :] += add
+
+    def chunk(k):
+        @pl.when(me == 0)
+        def _():
+            chain(table, 0, k, 2).wait_send()
+            chain(table, 0, k, 1).start()
+
+        for dev in (2, 6, 4, 1, 5, 7, 3):
+            half = dev % 2
+
+            @pl.when(me == dev)
+            def _(dev=dev, half=half):
+                if dev == 1:
+                    pass_on(table, half, k, 0).wait_recv()
+                else:
+                    chain(table, half, k, 0).wait_recv()
+                if dev in nxt:
+                    chain(hot, half, k, nxt[dev]).start()
+                if dev != 1:
+                    pass_on(hot, half, k, dev + 1 - 2 * half).start()
+
+        for u in range(N_DEV * per // CHUNKS):
+            listing(k * (N_DEV * per // CHUNKS) + u)
+
+    loop(CHUNKS, chunk)
+    own_ref[...] = own_f[...].astype(I32) - 1
+
+    @pl.when(me == 0)
+    def _():
+        root_copy().wait()
+        root_store().start()
+
+    def tail(k):
+        @pl.when(me == 0)
+        def _():
+            chain(table, 0, k, 1).wait_send()
+            pass_on(table, 1, k, 1).wait_send()
+
+        @pl.when(me == 1)
+        def _():
+            chain(table, 0, k, 0).wait_recv()
+            chain(hot, 1, k, 5).wait_send()
+
+        for dev in (2, 6, 4, 5, 7, 3):
+            half = dev % 2
+
+            @pl.when(me == dev)
+            def _(dev=dev, half=half):
+                pass_on(table, 1 - half, k, 0).wait_recv()
+                if dev in nxt:
+                    chain(hot, half, k, nxt[dev]).wait_send()
+                pass_on(hot, half, k, dev + 1 - 2 * half).wait_send()
+
+    loop(CHUNKS, tail)
+    for off in OTHERS:
+        pack_to(off).wait_send()
+
+    @pl.when(me == 0)
+    def _():
+        root_store().wait()
+
+
+CODE = 32768.0
+
+
+def prologue(pk, table):
+    dma = pltpu.SemaphoreType.DMA
+    per = TOK // LANE
+    vm = pl.BlockSpec(memory_space=pltpu.VMEM)
     return pl.pallas_call(
-        index_kernel,
-        grid_spec=pltpu.PrefetchScalarGridSpec(
-            num_scalar_prefetch=1,
-            grid=(1,),
-            in_specs=[full(1, TOK), full(TOK, 64)],
-            out_specs=[
-                full(TOK // LANE, LANE),
-                full(8, 256),
-                full(8, LANE),
-            ],
-            scratch_shapes=[pltpu.VMEM((TOK, 64), F32)],
-        ),
+        prologue_kernel,
+        in_specs=[vm, ANY],
+        out_specs=[ANY] + [vm] * 6,
         out_shape=[
-            shape_of(I32, TOK // LANE, LANE),
-            shape_of(I32, 8, 256),
-            shape_of(F32, 8, LANE),
+            shape_of(BF16, HOT, D),
+            shape_of(F32, N_DEV, PACK, LANE),
+            shape_of(I32, per, LANE),
+            shape_of(I32, per, LANE),
+            shape_of(I32, per, LANE),
+            shape_of(I32, N_DEV, 2 * LANE),
+            shape_of(F32, SUB, LANE),
         ],
-        compiler_params=params(),
-        cost_estimate=cost(5e9, 2e6),
-        name="index_maps",
-    )(me, mine, ids64)
+        scratch_shapes=[
+            pltpu.VMEM((N_DEV, PACK, LANE), F32),
+            pltpu.VMEM((LANE, N_DEV * per), F32),
+            pltpu.VMEM((N_DEV, 2 * LANE), F32),
+            pltpu.VMEM((HOT, D), BF16),
+            dma,
+            dma((N_DEV,)),
+            dma((N_DEV,)),
+        ]
+        + [dma((CHUNKS,))] * 4,
+        compiler_params=params(collective_id=0, has_side_effects=True),
+        cost_estimate=cost(8e10, 4e7),
+        name="prologue",
+    )(pk, table)
 
 
 def merge_kernel(row_ref, col_ref, tgt_ref, rep_ref):
@@ -188,7 +339,7 @@
     i = pl.program_id(0)
 
     def fetch(blk, slot):
-        def body(q, c):
+        def body(q):
             for u in range(8):
                 j = q * 8 + u
                 r = lax.shift_right_logical(jnp.maximum(idx_s[blk, j], 0), 1)
@@ -197,9 +348,8 @@
                     buf.at[slot, pl.ds(pl.multiple_of(j * 2, 2), 2), :],
                     sem.at[slot],
                 ).start()
-            return c
-
-        lax.fori_loop(0, n // 8, body, 0)
+
+        loop(n // 8, body)
 
     slot = lax.rem(i, 2)
 
@@ -211,10 +361,10 @@
     def _():
         fetch(i + 1, 1 - slot)
 
-    idx = jnp.maximum(idx_ref[pl.ds(i, 1), :][:, :n], 0)
+    idx = idx_ref[pl.ds(i, 1), :][:, :n]
     k_io = lax.broadcasted_iota(I32, (2 * n, n), 0)
     j_io = lax.broadcasted_iota(I32, (2 * n, n), 1)
-    want = 2 * j_io + jnp.bitwise_and(idx, 1)
+    want = jnp.where(idx < 0, -1, 2 * j_io + jnp.bitwise_and(idx, 1))
     pick = (k_io == want).astype(BF16)
     pltpu.make_async_copy(src_ref.at[pl.ds(0, 2 * n), :], buf.at[slot], sem.at[slot]).wait()
     out_ref[0] = dot(pick, buf[slot], TN).astype(BF16)
@@ -238,190 +388,44 @@
     )(idx, idx, src)
 
 
-CHUNKS = 8
-HALF = HOT // 2
-CH = HALF // CHUNKS
-
-
-def lookup_kernel(table, send, buf, stage, ld_sem, st_sem, a_send, a_recv, b_send, b_recv, d_send, d_recv, c_send, c_recv):
-    me = lax.axis_index("fsdp")
-    barrier = pltpu.get_barrier_semaphore()
-    for off in range(1, N_DEV):
-        pl.semaphore_signal(barrier, inc=1, device_id=(lax.rem(me + off, N_DEV),), device_id_type=MESH)
-    pl.semaphore_wait(barrier, N_DEV - 1)
-
-    def a_rows(k):
-        return pl.ds(k * CH, CH)
-
-    def b_rows(k):
-        return pl.ds(HALF + k * CH, CH)
-
-    def remote(src, rows, s_sem, r_sem, dev):
-        return pltpu.make_async_remote_copy(src_ref=src.at[rows, :], dst_ref=buf.at[rows, :], send_sem=s_sem, recv_sem=r_sem, device_id=(dev,), device_id_type=MESH)
-
-    def cold(off):
-        dst = lax.rem(me + off, N_DEV)
-        return pltpu.make_async_remote_copy(
-            src_ref=send.at[dst],
-            dst_ref=buf.at[pl.ds(pl.multiple_of(HOT + me * CAP, 16), CAP), :],
-            send_sem=c_send.at[off],
-            recv_sem=c_recv.at[off],
-            device_id=(dst,),
-            device_id_type=MESH,
-        )
-
-    def cold_in(off):
-        src = lax.rem(me - off + N_DEV, N_DEV)
-        return pltpu.make_async_remote_copy(
-            src_ref=send.at[0],
-            dst_ref=buf.at[pl.ds(pl.multiple_of(HOT + src * CAP, 16), CAP), :],
-            send_sem=c_send.at[off],
-            recv_sem=c_recv.at[off],
-            device_id=(src,),
-            device_id_type=MESH,
-        )
-
-    root = me == 0
-    nxt = {2: 6, 6: 4, 1: 5, 5: 7, 7: 3}
-    for k in range(CHUNKS):
-
-        @pl.when(root)
-        def _(k=k):
-            remote(table, a_rows(k), a_send.at[k], a_recv.at[k], 2).start()
-            remote(table, b_rows(k), b_send.at[k], b_recv.at[k], 1).start()
-            remote(table, a_rows(k), d_send.at[k], d_recv.at[k], 1).start()
-
-        for dev in (2, 6, 4):
-
-            @pl.when(me == dev)
-            def _(k=k, dev=dev):
-                remote(table, a_rows(k), a_send.at[k], a_recv.at[k], 0).wait_recv()
-                if dev in nxt:
-                    remote(buf, a_rows(k), a_send.at[k], a_recv.at[k], nxt[dev]).start()
-                remote(buf, a_rows(k), d_send.at[k], d_recv.at[k], dev + 1).start()
-
-        for dev in (1, 5, 7, 3):
-
-            @pl.when(me == dev)
-            def _(k=k, dev=dev):
-                remote(table, b_rows(k), b_send.at[k], b_recv.at[k], 0).wait_recv()
-                if dev in nxt:
-                    remote(buf, b_rows(k), b_send.at[k], b_recv.at[k], nxt[dev]).start()
-                if dev != 1:
-                    remote(buf, b_rows(k), d_send.at[k], d_recv.at[k], dev - 1).start()
-
-        if 1 <= k + 1 < N_DEV:
-            cold(k + 1).start()
-
-    ld = pltpu.make_async_copy(send.at[me], stage.at[pl.ds(0, CAP), :], ld_sem)
-    ld.start()
-    ld.wait()
-    st = pltpu.make_async_copy(stage.at[pl.ds(0, CAP), :], buf.at[pl.ds(pl.multiple_of(HOT + me * CAP, 16), CAP), :], st_sem)
-    st.start()
-    st.wait()
-
-    @pl.when(root)
-    def _():
-        big = pltpu.make_async_copy(table.at[pl.ds(0, HOT), :], stage, ld_sem)
-        big.start()
-        big.wait()
-        out = pltpu.make_async_copy(stage, buf.at[pl.ds(0, HOT), :], st_sem)
-        out.start()
-        out.wait()
-
-    for k in range(CHUNKS):
-        for dev in (1, 3, 5, 7):
-
-            @pl.when(me == dev)
-            def _(k=k):
-                remote(table, a_rows(k), d_send.at[k], d_recv.at[k], 0).wait_recv()
-
-        for dev in (2, 4, 6):
-
-            @pl.when(me == dev)
-            def _(k=k):
-                remote(table, b_rows(k), d_send.at[k], d_recv.at[k], 0).wait_recv()
-
-    for off in range(1, N_DEV):
-        cold_in(off).wait_recv()
-    for off in range(1, N_DEV):
-        cold(off).wait_send()
-    for k in range(CHUNKS):
-
-        @pl.when(root)
-        def _(k=k):
-            remote(table, a_rows(k), a_send.at[k], a_recv.at[k], 2).wait_send()
-            remote(table, b_rows(k), b_send.at[k], b_recv.at[k], 1).wait_send()
-            remote(table, a_rows(k), d_send.at[k], d_recv.at[k], 1).wait_send()
-
-        for dev in (2, 6, 4):
-
-            @pl.when(me == dev)
-            def _(k=k, dev=dev):
-                if dev in nxt:
-                    remote(buf, a_rows(k), a_send.at[k], a_recv.at[k], nxt[dev]).wait_send()
-                remote(buf, a_rows(k), d_send.at[k], d_recv.at[k], dev + 1).wait_send()
-
-        for dev in (1, 5, 7, 3):
-
-            @pl.when(me == dev)
-            def _(k=k, dev=dev):
-                if dev in nxt:
-                    remote(buf, b_rows(k), b_send.at[k], b_recv.at[k], nxt[dev]).wait_send()
-                if dev != 1:
-                    remote(buf, b_rows(k), d_send.at[k], d_recv.at[k], dev - 1).wait_send()
-
-
-def lookup_exchange(table, send):
-    dma = pltpu.SemaphoreType.DMA
-    return pl.pallas_call(
-        lookup_kernel,
-        in_specs=[ANY] * 2,
-        out_specs=ANY,
-        out_shape=shape_of(BF16, BUF, D),
-        scratch_shapes=[pltpu.VMEM((HOT, D), BF16), dma, dma] + [dma((CHUNKS,))] * 6 + [dma((N_DEV,))] * 2,
-        compiler_params=params(collective_id=0, has_side_effects=True),
-        cost_estimate=cost(8e10, 4e7),
-        name="lookup_exchange",
-    )(table, send)
-
-
-def proj_kernel(x_ref, gain_ref, w_ref, bias_ref, cos_ref, sin_ref, hid_ref, qkv_ref):
-    x = x_ref[...].astype(F32)
+def proj_kernel(xh_ref, slot_ref, cold_ref, gain_ref, w_ref, bias_ref, cos_ref, sin_ref, x_ref, hid_ref, qkv_ref):
+    tm = xh_ref.shape[0]
+    picked = []
+    for b in range(tm // LANE):
+        slot = slot_ref[pl.ds(pl.program_id(0) * (tm // LANE) + b, 1), :]
+        pick = (iota(I32, (COLD, LANE), 0) == slot).astype(F32).astype(BF16)
+        picked.append(dot(pick, cold_ref[...], TN))
+    x = xh_ref[...].astype(F32) + jnp.concatenate(picked, axis=0)
+    x_ref[...] = x.astype(BF16)
     inv = lax.rsqrt(row_mean(x * x) + NORM_EPS)
     hid = (x * inv * gain_ref[...]).astype(BF16)
     hid_ref[...] = hid
     cos_t = cos_ref[...]
     sin_t = sin_ref[...]
-    for c in range(0, QKV, 512):
-        lin = dot(hid, w_ref[:, c : c + 512], NN) + bias_ref[:, c : c + 512]
-        for h in range(0, 512, HEAD_DIM):
+    wide = 4 * HEAD_DIM
+    for c in range(0, QKV, wide):
+        lin = dot(hid, w_ref[:, c : c + wide], NN) + bias_ref[:, c : c + wide]
+        for h in range(0, wide, HEAD_DIM):
             v = lin[:, h : h + HEAD_DIM]
             if c + h < D + KV * HEAD_DIM:
                 v = v * cos_t + pltpu.roll(v, HEAD_DIM // 2, 1) * sin_t
             qkv_ref[:, c + h : c + h + HEAD_DIM] = v.astype(BF16)
 
 
-def proj(x, gain, w, bias, cos_t, sin_t):
-    tm = 256
+def proj(xh, slot, cold, gain, w, bias, cos_t, sin_t):
+    tm = 2 * LANE
     per = SEQ // tm
+    turn = pl.BlockSpec((tm, HEAD_DIM), lambda i: (lax.rem(i, per), 0))
     return pl.pallas_call(
         proj_kernel,
         grid=(TOK // tm,),
-        in_specs=[
-            by_row(tm, D),
-            full(1, D),
-            full(D, QKV),
-            full(1, QKV),
-            pl.BlockSpec((tm, HEAD_DIM), lambda i: (lax.rem(i, per), 0)),
-            pl.BlockSpec((tm, HEAD_DIM), lambda i: (lax.rem(i, per), 0)),
-        ],
-        out_specs=[by_row(tm, D), by_row(tm, QKV)],
-        out_shape=[shape_of(BF16, TOK, D), shape_of(BF16, TOK, QKV)],
+        in_specs=[by_row(tm, D), full(*slot.shape), full(COLD, D), full(1, D), full(D, QKV), full(1, QKV), turn, turn],
+        out_specs=[by_row(tm, D), by_row(tm, D), by_row(tm, QKV)],
+        out_shape=[shape_of(BF16, TOK, D), shape_of(BF16, TOK, D), shape_of(BF16, TOK, QKV)],
         compiler_params=params(),
-        cost_estimate=cost(2 * TOK * D * QKV, 3e7),
+        cost_estimate=cost(2 * TOK * D * (QKV + COLD), 3e7),
         name="proj",
-    )(x, gain, w, bias, cos_t, sin_t)
+    )(xh, slot, cold, gain, w, bias, cos_t, sin_t)
 
 
 QB = 256
@@ -596,20 +600,18 @@
 
     @pl.when(i == 0)
     def _():
-        def zero(b, c):
+        def zero(b):
             acc[pl.ds(pl.multiple_of(b * LANE, LANE), LANE), :] = jnp.zeros((LANE, D), F32)
-            return c
-
-        lax.fori_loop(0, BUF // LANE, zero, 0)
-
-    def body(q, c):
+
+        loop(BUF // LANE, zero)
+
+    def body(q):
         for u in range(8):
             t = q * 8 + u
             r = xi_s[i * (tm // LANE) + lax.shift_right_logical(t, 7), jnp.bitwise_and(t, 127)]
             acc[pl.ds(r, 1), :] += dx_ref[pl.ds(t, 1), :]
-        return c
-
-    lax.fori_loop(0, tm // 8, body, 0)
+
+    loop(tm // 8, body)
 
     @pl.when(i == pl.num_programs(0) - 1)
     def _():
@@ -639,6 +641,134 @@
     )(xi, dx)
 
 
+PIECES = 32
+
+
+def reduce_kernel(hot, cold, out_hot, out_cold, mine, pair, above, done, stage, l_sem, s_sem, x_send, x_recv, c_send, c_recv, h_send, h_recv, o_sem, o_recv):
+    me = lax.axis_index("fsdp")
+    half = mine.shape[0]
+    n = half // PIECES
+    core = lax.rem(me, 2)
+    other = me + 1 - 2 * core
+    meet(me)
+
+    def part(ref, k):
+        return rows_of(ref, k * n, n)
+
+    def load(k):
+        return pltpu.make_async_copy(rows_of(hot, core * half + k * n, n), part(mine, k), l_sem.at[k])
+
+    def trade(k):
+        return push(rows_of(hot, (1 - core) * half + k * n, n), part(pair, k), x_send.at[k], x_recv.at[k], other)
+
+    def cold_to(off):
+        dst = lax.rem(me + off, N_DEV)
+        return push(cold.at[dst], out_cold.at[me], c_send.at[off], c_recv.at[off], dst)
+
+    def cold_from(off):
+        src = lax.rem(me - off + N_DEV, N_DEV)
+        return push(cold.at[0], out_cold.at[src], c_send.at[off], c_recv.at[off], src)
+
+    def hand(k, dev):
+        return push(part(mine, k), part(above, k), h_send.at[k], h_recv.at[k], dev)
+
+    def keep(k):
+        return pltpu.make_async_copy(part(done, k), part(out_hot, k), o_sem.at[k])
+
+    def give(k):
+        return push(part(done, k), rows_of(out_hot, half + k * n, n), o_sem.at[k], o_recv.at[k], 0)
+
+    def begin(k):
+        load(k).start()
+        trade(k).start()
+
+    loop(PIECES, begin)
+    for off in OTHERS:
+        cold_to(off).start()
+    own_in = pltpu.make_async_copy(cold.at[me], stage, s_sem)
+    own_in.start()
+    own_in.wait()
+    own_out = pltpu.make_async_copy(stage, out_cold.at[me], s_sem)
+    own_out.start()
+    nxt = {4: 6, 6: 2, 2: 0, 3: 7, 7: 5, 5: 1}
+    head = jnp.logical_or(me == 4, me == 3)
+    end = me < 2
+
+    def step(k):
+        rows = pl.ds(pl.multiple_of(k * n, SUB), n)
+        load(k).wait()
+        trade(k).wait_recv()
+
+        @pl.when(head)
+        def _():
+            mine[rows, :] = mine[rows, :] + pair[rows, :]
+
+        @pl.when(jnp.logical_not(head))
+        def _():
+            hand(k, 0).wait_recv()
+            mine[rows, :] = mine[rows, :] + pair[rows, :] + above[rows, :]
+
+        for dev, to in nxt.items():
+
+            @pl.when(me == dev)
+            def _(to=to):
+                hand(k, to).start()
+
+        @pl.when(end)
+        def _():
+            done[rows, :] = mine[rows, :].astype(BF16)
+
+        @pl.when(me == 0)
+        def _():
+            keep(k).start()
+
+        @pl.when(me == 1)
+        def _():
+            give(k).start()
+
+    loop(PIECES, step)
+
+    def tail(k):
+        trade(k).wait_send()
+
+        @pl.when(jnp.logical_not(end))
+        def _():
+            hand(k, 0).wait_send()
+
+        @pl.when(me == 0)
+        def _():
+            keep(k).wait()
+            give(k).wait_recv()
+
+        @pl.when(me == 1)
+        def _():
+            give(k).wait_send()
+
+    loop(PIECES, tail)
+    own_out.wait()
+    for off in OTHERS:
+        cold_from(off).wait_recv()
+        cold_to(off).wait_send()
+
+
+def reduce_rows(hot, cold):
+    dma = pltpu.SemaphoreType.DMA
+    half = hot.shape[0] // 2
+    many = dma((PIECES,))
+    dev = dma((N_DEV,))
+    return pl.pallas_call(
+        reduce_kernel,
+        in_specs=[ANY, ANY],
+        out_specs=[ANY, ANY],
+        out_shape=[shape_of(BF16, *hot.shape), shape_of(cold.dtype, *cold.shape)],
+        scratch_shapes=[pltpu.VMEM((half, D), F32)] * 3
+        + [pltpu.VMEM((half, D), BF16), pltpu.VMEM(cold.shape[1:], cold.dtype), many, dma, many, many, dev, dev, many, many, many, many],
+        compiler_params=params(collective_id=3, has_side_effects=True),
+        cost_estimate=cost(8e10, 4e7),
+        name="reduce_rows",
+    )(hot, cold)
+
+
 ZROWS = 512
 
 
@@ -668,11 +798,10 @@
         for lo in range(0, HOT, ZROWS):
             fill(lo, ZROWS).start()
 
-    def clear(b, c):
+    def clear(b):
         acc[pl.ds(pl.multiple_of(b * LANE, LANE), LANE), :] = jnp.zeros((LANE, D), F32)
-        return c
-
-    lax.fori_loop(0, 2 * COLD // LANE, clear, 0)
+
+    loop(2 * COLD // LANE, clear)
 
     @pl.when(me == 0)
     def _():
@@ -681,21 +810,19 @@
 
     pltpu.make_async_copy(cold_ref, cold, c_sem).wait()
 
-    def add(q, c):
+    def add(q):
         for u in range(8):
             j = q * 8 + u
             r = tgt_s[lax.shift_right_logical(j, 7), jnp.bitwise_and(j, 127)]
             acc[pl.ds(r, 1), :] += cold[pl.ds(j, 1), :]
-        return c
-
-    lax.fori_loop(0, COLD // 8, add, 0)
-
-    def conv(b, c):
+
+    loop(COLD // 8, add)
+
+    def conv(b):
         rows = pl.ds(pl.multiple_of(b * LANE, LANE), LANE)
         stage[rows, :] = acc[rows, :].astype(BF16)
-        return c
-
-    lax.fori_loop(0, 2 * COLD // LANE, conv, 0)
+
+    loop(2 * COLD // LANE, conv)
 
     for lo, n in spans:
         fill(lo, n).wait()
@@ -728,11 +855,10 @@
 
     count = lax.fori_loop(0, COLD, put, jnp.int32(0))
 
-    def drain(j, c):
+    def drain(j):
         pair_copy(0, 0).wait()
-        return c
-
-    lax.fori_loop(0, count, drain, 0)
+
+    loop(count, drain)
 
 
 def final_rows(me, own, tgt, rep, hot, cold):
@@ -766,7 +892,7 @@
 def swap_kernel(same, x_ref, out_ref, own_sem, send_sem, recv_sem):
     me = lax.axis_index("fsdp")
     barrier = pltpu.get_barrier_semaphore()
-    for off in range(1, N_DEV):
+    for off in OTHERS:
         pl.semaphore_signal(barrier, inc=1, device_id=(lax.rem(me + off, N_DEV),), device_id_type=MESH)
     pl.semaphore_wait(barrier, N_DEV - 1)
 
@@ -792,14 +918,14 @@
             device_id_type=MESH,
         )
 
-    for off in range(1, N_DEV):
+    for off in OTHERS:
         copy(off).start()
     own = pltpu.make_async_copy(x_ref.at[0 if same else me], out_ref.at[me], own_sem)
     own.start()
     own.wait()
-    for off in range(1, N_DEV):
+    for off in OTHERS:
         inward(off).wait_recv()
-    for off in range(1, N_DEV):
+    for off in OTHERS:
         copy(off).wait_send()
 
 
@@ -857,66 +983,62 @@
     me1 = me.reshape(1).astype(I32)
     first = me * ROWS
     kvw = KV * HEAD_DIM
-    mine = tok_ids.reshape(1, TOK).astype(F32)
-    small = jnp.concatenate([mine[0]] + [v.astype(F32) for v in (gain_p, bq_p, bk_p, bv_p)])
-    small = lax.all_gather(small, ax)
-    w_qkv = lax.all_gather(jnp.concatenate([wq_p, wk_p, wv_p], axis=1), ax, axis=0, tiled=True)
+    w_in = jnp.concatenate([wq_p, wk_p, wv_p], axis=1)
+    w_in, wo_p = lax.optimization_barrier((w_in, wo_p))
+    w_qkv = lax.all_gather(w_in, ax, axis=0, tiled=True)
     w_out = lax.all_gather(wo_p, ax, axis=0, tiled=True)
-    ids_f = small[:, :TOK]
-    cuts = [TOK, TOK + D // N_DEV, TOK + 2 * (D // N_DEV), TOK + 2 * (D // N_DEV) + kvw // N_DEV, TOK + 2 * (D // N_DEV) + 2 * (kvw // N_DEV)]
-    gain, b_q, b_k, b_v = (small[:, a:b].reshape(1, -1) for a, b in zip(cuts[:-1], cuts[1:], strict=True))
-    bias = jnp.concatenate([b_q, b_k, b_v], axis=1)
+    small = [v.astype(F32) for v in (gain_p, bq_p, bk_p, bv_p)]
+    size = [v.shape[0] for v in small]
+    fill = PACK * LANE - TOK - sum(size)
+    pk = jnp.concatenate([tok_ids.astype(F32).reshape(-1)] + small + [jnp.zeros(fill, F32)]).reshape(PACK, LANE)
+    hot_rows, every, xi, hid_idx, slot, own, most = prologue(pk, table)
+    every = every.reshape(N_DEV, -1)
+    ids = every[:, :TOK].astype(I32)
+    over = most[0, 0] > CAP
+    vecs, at = [], TOK
+    for n in size:
+        vecs.append(every[:, at : at + n].reshape(1, -1))
+        at += n
+    gain = vecs[0]
+    bias = jnp.concatenate(vecs[1:], axis=1)
     cos_t, sin_t = rope_tables()
 
-    xi, own, most = index_maps(me1, mine, jnp.repeat(ids_f.T, N_DEV, axis=1))
-    over = most[0, 0] > CAP
-    send = gather_rows(table, own, CAP)
-    buf = lookup_exchange(table, send)
-    x = lax.cond(
+    cold_x = lax.all_to_all(gather_rows(table, own, CAP), ax, 0, 0, tiled=True).reshape(COLD, D)
+    xh, slot_x = lax.cond(
         over,
-        lambda: general_lookup(table, ids_f.astype(I32), first).reshape(TOK, D),
-        lambda: gather_rows(buf, xi, LANE).reshape(TOK, D),
+        lambda: (general_lookup(table, ids, first), jnp.full_like(slot, -1)),
+        lambda: (gather_rows(hot_rows, hid_idx, LANE).reshape(TOK, D), slot),
     )
-    x = lax.optimization_barrier(x)
     go = grad_out.reshape(TOK, D)
-
-    hid, qkv = proj(x, gain, w_qkv, bias, cos_t, sin_t)
     d_attn = dot(go, w_out, NT).astype(BF16)
+    x, hid, qkv = proj(xh, slot_x, cold_x, gain, w_qkv, bias, cos_t, sin_t)
     attn, dq, dk, dv, s_q, s_k, s_v = attention(qkv, d_attn, cos_t, sin_t)
+    gw_out = dot(attn, go, TN)
+    gw_out, dq = lax.optimization_barrier((gw_out, dq))
+    g_out = lax.psum_scatter(gw_out, ax, scatter_dimension=0, tiled=True)
+    gw_qkv = qkv_weight_grad(hid, dq, dk, dv)
+    gw_qkv, dq, dk, dv = lax.optimization_barrier((gw_qkv, dq, dk, dv))
+    g_qkv = lax.psum_scatter(gw_qkv, ax, scatter_dimension=0, tiled=True)
+    d_x, s_g = input_grad(dq, dk, dv, w_qkv, x, go, gain)
     block_out = (x.astype(F32) + dot(attn, w_out, NN)).astype(BF16).reshape(grad_out.shape)
-    g_out = lax.psum_scatter(dot(attn, go, TN), ax, scatter_dimension=0, tiled=True)
-    d_x, s_g = input_grad(dq, dk, dv, w_qkv, x, go, gain)
-    g_qkv = lax.psum_scatter(qkv_weight_grad(hid, dq, dk, dv), ax, scatter_dimension=0, tiled=True)
 
     parts = [s_g.sum(0), s_q.sum((0, 1)), s_k.sum((0, 1)), s_v.sum((0, 1))]
     vec = jnp.concatenate([p.reshape(N_DEV, -1) for p in parts], axis=1)
     vec = lax.all_to_all(vec, ax, 0, 0, tiled=True).sum(0)
 
     hot, cold = scatter_rows(xi, d_x)
-    cold = lax.all_to_all(cold.reshape(N_DEV, CAP, D), ax, 0, 0, tiled=True).reshape(COLD, D)
-    hot = lax.psum_scatter(hot, ax, scatter_dimension=0, tiled=True).astype(BF16)
-    hot = lax.all_gather(hot, ax, axis=0, tiled=True)
+    hot, cold = reduce_rows(hot, cold.reshape(N_DEV, CAP, D))
     flat = own[:, :CAP].reshape(1, COLD).astype(F32)
     tgt, rep = merge_maps(flat, flat.reshape(COLD, 1))
     grad_table = lax.cond(
         over,
-        lambda: general_scatter(d_x, ids_f.astype(I32), first),
-        lambda: final_rows(me1, own, tgt, rep, hot, cold),
+        lambda: general_scatter(d_x, ids, first),
+        lambda: final_rows(me1, own, tgt, rep, hot, cold.reshape(COLD, D)),
     )
-
-    e0, e1, e2 = D // N_DEV, 2 * (D // N_DEV), 2 * (D // N_DEV) + kvw // N_DEV
-    return (
-        block_out,
-        grad_table,
-        vec[:e0],
-        g_qkv[:, :D],
-        vec[e0:e1],
-        g_qkv[:, D : D + kvw],
-        vec[e1:e2],
-        g_qkv[:, D + kvw :],
-        vec[e2:],
-        g_out,
-    )
+    cut = [sum(size[:i]) for i in range(len(size) + 1)]
+    g_gain, g_bq, g_bk, g_bv = (vec[a:b] for a, b in zip(cut[:-1], cut[1:], strict=True))
+    g_q, g_k, g_v = g_qkv[:, :D], g_qkv[:, D : D + kvw], g_qkv[:, D + kvw :]
+    return block_out, grad_table, g_gain, g_q, g_bq, g_k, g_bk, g_v, g_bv, g_out
 
 
 def solution(mesh):

time: 1010 us -> 879 us (0.87)
  waiting for transfers between devices: 385 us -> 0.76 us
  Pallas kernels: 506 us -> 778 us
    reduce_scatter x3 -> x2, waiting for transfers between devices: 283 us -> 0.01 us  [the longest x1 0.01 us: device_step(): g_qkv = lax.psum_scatter(gw_qkv, ax, scatter_dimension=0, tiled=True)]
    pallas_call x2, Pallas kernels: 176 us -> 422 us  [the longest x1 300 us: reduce_rows(): pl.pallas_call(reduce_kernel, in_specs=[ANY, ANY], out_specs=[ANY, ANY],...]
    all_gather x2 -> x1, waiting for transfers between devices: 63.7 us -> 0.01 us  [device_step(): w_qkv = lax.all_gather(w_in, ax, axis=0, tiled=True)]
    unnamed x8 -> x4, waiting for transfers between devices: 38.9 us -> 0.75 us
    pallas_call x2, Pallas kernels: 54.6 us -> 69.4 us  [gather_rows(): pl.pallas_call(functools.partial(gather_kernel, n), grid_spec=pltpu.Prefe...]
    pallas_call x1, Pallas kernels: 20.9 us -> 32.4 us  [proj(): pl.pallas_call(proj_kernel, grid=(TOK // tm,), in_specs=[by_row(tm, D), f...]
  transfers between devices with their start and end apart: 8 -> 6, of which waited for: 5 -> 0; matrix products, arithmetic and copies ran while one was open for 7% -> 6% of each run, Pallas kernels for 32% -> 70%
where the time goes in v2:
time: 879 us; the launch traced here: 875 us
  Pallas kernels  778 us (89%)
  matrix products  46.9 us (5%)
  local copies, waits for them, and re-layouts  15 us (2%)
  between operations  14.6 us (2%)
  starting transfers between devices  10.8 us (1%)
    pallas_call x1, Pallas kernels, reduce_rows(): pl.pallas_call(reduce_kernel, in_specs=[ANY, ANY], out_specs=[ANY, ANY],...  300 us
    pallas_call x1, Pallas kernels, prologue(): pl.pallas_call(prologue_kernel, in_specs=[vm, ANY], out_specs=[ANY] + [vm...  122 us
    pallas_call x1, Pallas kernels, attention(): pl.pallas_call(attn_kernel, grid=(SEQS, KV, GROUP), in_specs=[pl.BlockSpe...  111 us
    pallas_call x2, Pallas kernels, gather_rows(): pl.pallas_call(functools.partial(gather_kernel, n), grid_spec=pltpu.Prefe...  69.4 us
    pallas_call x1, Pallas kernels, final_rows(): pl.pallas_call(final_kernel, grid_spec=pltpu.PrefetchScalarGridSpec(num_s...  66.9 us
    dot_general x3, matrix products, dot(): return lax.dot_general(a, b, (dims, ((), ())), preferred_element_type=F32)  46.9 us
    pallas_call x1, Pallas kernels, proj(): pl.pallas_call(proj_kernel, grid=(TOK // tm,), in_specs=[by_row(tm, D), f...  32.4 us
    pallas_call x1, Pallas kernels, scatter_rows(): pl.pallas_call(scatter_kernel, grid_spec=pltpu.PrefetchScalarGridSpec(num...  30.5 us
  transfers between devices with their start and end apart: 6, of which 0 were waited for; matrix products, arithmetic and copies ran while one was open for 6% of the time, Pallas kernels for 70%

profile of v2, /device:TPU:0, one launch (start us, length us, event | category | flops | bytes accessed | tf_op | source)
XLA Modules:
  0.0 874.9 jit_solution(1060249006301305871)
XLA Ops:
  7.2 0.0 all-gather.5.cloned.1.call-start
  7.2 2.2 pad_maximum_fusion
  9.4 0.0 all-gather.5.cloned.1.call-update
  9.4 0.0 all-gather.3.cloned.1.call-start
  9.4 0.7 all-gather.3.cloned.1.call-update
  10.2 0.7 convert_bitcast_fusion
  10.9 3.3 concatenate.18
  14.2 122.4 %prologue.1 = (bf16[4096,1536]{1,0:T(8,128)(2,1)}, f32[8,20,128]{2,1,0:T(8,128)}, s32[16,128]{1,0:T(8,128)}, s32[16,128]{1,0:T(8,128)S(1)}, s32[16,128]{1,0:T(8,...) custom-call(f32[20,128]{1,0:T(8,128)} %bitcast.55, bf16[18992,1536]{1,0:T(8,128)(2,1)} %src_ref.1), custom_call_target="tpu_custom_call" | custom-call | flops 80000000000 | bytes 40000000 | tf_op jit(solution)/shard_map/prologue/pallas_call | solution.py:281
  136.6 0.0 copy-start.5
  136.6 27.9 %gather_rows.3 = bf16[8,176,1536]{2,1,0:T(8,128)(2,1)} custom-call(s32[8,256]{1,0:T(8,128)S(1)} %get-tuple-element.327.idx_s.idx_ref, s32[8,256]{1,0:T(8,128)S(1)} %get-tuple-element.327.idx_s.idx_ref, bf16[18992,1536]{1,0:T(8,128)(2,1)} %src_ref.1), custom_call_target="tpu_custom_call" | custom-call | flops 20000000000 | bytes 12976128 | tf_op jit(solution)/shard_map/gather_rows/pallas_call | solution.py:375
  164.5 0.0 copy-done.5
  164.5 0.0 copy-start.2
  164.5 7.3 all-to-all-start
  171.8 0.0 reduce-scatter.3.cloned.1.call-start
  171.8 1.2 slice.42
  173.7 0.1 fusion.6
  173.8 0.1 reshape.167
  173.8 0.1 reshape.168
  173.9 0.1 fusion.5
  174.0 0.1 reshape.166
  174.1 0.7 reshape.165.gain_ref
  174.8 0.6 copy-done
  175.4 41.5 %conditional.2 = (bf16[2048,1536]{1,0:T(8,128)(2,1)}, s32[16,128]{1,0:T(8,128)S(1)}) conditional(s32[]{:T(128)} %bitcast.10, (s32[16,128]{1,0:T(8,128)S(1)}, bf16[4096,1536]{1,0:T(8,128)(2,1)}, s32[16,128]{1,0:T(8,128)S(1)}) %tuple.61, (s32[8,2048]{1,0:T(8,128)S(1)}, s32[]{:T(128)}, bf16[18992,1536]{1,0:T(8,128)(2,1)}) %tuple.62), branch_computations={%region_0.0_spmd, %region_1.5_spmd} | conditional | flops 20000000000 | bytes 23229718 | solution.py:1007
  175.4 41.5 %gather_rows.2 = bf16[16,128,1536]{2,1,0:T(8,128)(2,1)} custom-call(s32[16,128]{1,0:T(8,128)S(1)} %get-tuple-element.246.idx_s.idx_ref, s32[16,128]{1,0:T(8,128)S(1)} %get-tuple-element.246.idx_s.idx_ref, bf16[4096,1536]{1,0:T(8,128)(2,1)} %get-tuple-element.247.src_ref), custom_call_target="tpu_custom_call" | custom-call | flops 20000000000 | bytes 18874368 | tf_op jit(solution)/shard_map/cond/branch_0_fun/gather_rows/pallas_call | solution.py:375
  216.9 2.0 fusion.3
  218.9 1.4 pad_maximum_fusion.1
  220.3 0.6 pad_maximum_fusion.4.bias_ref
  220.9 15.1 %fusion.do_ref = bf16[2048,1536]{1,0:T(8,128)(2,1)} fusion(bf16[1536,1536]{1,0:T(8,128)(2,1)} %all-gather.5.cloned.1.call-done, bf16[2048,1536]{1,0:T(8,128)(2,1)} %bitcast.56), kind=kOutput, calls=%fused_computation.15 | convolution fusion | flops 9666822144 | bytes 17301504 | tf_op jit(solution)/shard_map/dot_general | solution.py:88
  236.0 0.0 all-to-all-done
  236.0 32.4 %proj.1 = (bf16[2048,1536]{1,0:T(8,128)(2,1)}, bf16[2048,1536]{1,0:T(8,128)(2,1)}, bf16[2048,2048]{1,0:T(8,128)(2,1)}) custom-call(bf16[2048,1536]{1,0:T(8,128)(2,1)} %get-tuple-element.325.xh_ref, s32[16,128]{1,0:T(8,128)S(1)} %get-tuple-element.326.slot_ref, bf16[1408,1536]{1,0:T(8,128)(2,1)} %bitcast.11.cold_ref, f32[1,1536]{1,0:T(1,128)} %reshape.165.gain_ref, ...), custom_call_target="tpu_custom_call" | custom-call | flops 21743271936 | bytes 30000000 | tf_op jit(solution)/shard_map/proj/pallas_call | solution.py:419
  268.5 110.8 %attention.1 = (bf16[2048,1536]{1,0:T(8,128)(2,1)}, bf16[2048,1536]{1,0:T(8,128)(2,1)}, bf16[2048,256]{1,0:T(8,128)(2,1)}, bf16[2048,256]{1,0:T(8,128)(2,1)}, f3...) custom-call(bf16[2048,2048]{1,0:T(8,128)(2,1)} %get-tuple-element.330.q_ref.k_ref.v_ref, ...), custom_call_target="tpu_custom_call" | custom-call | flops 38654705664 | bytes 30000000 | tf_op jit(solution)/shard_map/attention/pallas_call | solution.py:493
  379.3 15.8 %fusion.9 = f32[1536,1536]{1,0:T(8,128)} fusion(bf16[2048,1536]{1,0:T(8,128)(2,1)} %get-tuple-element.332, bf16[2048,1536]{1,0:T(8,128)(2,1)} %bitcast.57), kind=kOutput, calls=%fused_computation.36 | convolution fusion | flops 9663676416 | bytes 22020096 | tf_op jit(solution)/shard_map/dot_general | solution.py:88
  395.1 19.2 %qkv_weight_grad.1 = f32[1536,2048]{1,0:T(8,128)} custom-call(bf16[2048,1536]{1,0:T(8,128)(2,1)} %get-tuple-element.334.h_ref, bf16[2048,1536]{1,0:T(8,128)(2,1)} %get-tuple-element.339.dq_ref, bf16[2048,256]{1,0:T(8,128)(2,1)} %get-tuple-element.340.dk_ref, bf16[2048,256]{1,0:T(8,128)(2,1)} %get-tuple-element.341.dv_ref), custom_call_target="tpu_custom_call" | custom-call | flops 12884901888 | bytes 30000000 | tf_op jit(solution)/shard_map/qkv_weight_grad/pallas_call | solution.py:585
  414.3 0.0 reduce-scatter.3.cloned.1.call-update
  414.3 0.0 reduce-scatter.5.cloned.1.call-start
  414.4 0.6 copy-done.6
  415.0 0.7 convert_element_type.65.row_ref
  415.7 1.1 convert_element_type.68.col_ref
  416.8 3.3 merge_maps.1
  420.1 0.0 reduce-scatter.5.cloned.1.call-update
  420.1 0.0 copy-start.4
  420.1 0.0 copy-start.3
  420.1 0.0 copy-start.1
  420.1 23.8 %input_grad.1 = (f32[2048,1536]{1,0:T(8,128)}, f32[8,1536]{1,0:T(8,128)}) custom-call(bf16[2048,1536]{1,0:T(8,128)(2,1)} %get-tuple-element.339.dq_ref, bf16[2048,256]{1,0:T(8,128)(2,1)} %get-tuple-element.340.dk_ref, bf16[2048,256]{1,0:T(8,128)(2,1)} %get-tuple-element.341.dv_ref, bf16[1536,2048]{1,0:T(8,128)(2,1)} %all-gather.3.cloned.1.call-done.w_ref, ...), custom_call_target="tpu_custom_call" | custom-call | flops 12884901888 | bytes 40000000 | tf_op jit(solution)/shard_map/input_grad/pallas_call | solution.py:553
  444.0 0.1 reshape.175
  444.1 0.1 reshape.174
  444.2 0.0 copy-done.1
  444.2 0.1 reshape.173
  444.3 0.8 reduce_sum.59
  445.1 0.1 reshape.172
  445.1 0.1 pad_maximum_fusion.3
  445.2 0.6 all_to_all.10
  445.8 3.3 all-to-all-start.1
  449.2 30.5 %scatter_rows.1 = (f32[4096,1536]{1,0:T(8,128)}, f32[1408,1536]{1,0:T(8,128)}) custom-call(s32[16,128]{1,0:T(8,128)} %get-tuple-element.333.xi_s, f32[2048,1536]{1,0:T(8,128)} %get-tuple-element.342.dx_ref), custom_call_target="tpu_custom_call" | custom-call | flops 30000001024 | bytes 50000000 | tf_op jit(solution)/shard_map/scatter_rows/pallas_call | solution.py:628
  479.7 299.7 %reduce_rows.1 = (bf16[4096,1536]{1,0:T(8,128)(2,1)}, f32[8,176,1536]{2,1,0:T(8,128)}) custom-call(f32[4096,1536]{1,0:T(8,128)} %get-tuple-element.343.hot, f32[8,176,1536]{2,1,0:T(8,128)} %bitcast.61), custom_call_target="tpu_custom_call" | custom-call | flops 80000000000 | bytes 40000000 | tf_op jit(solution)/shard_map/reduce_rows/pallas_call | solution.py:759
  779.3 16.0 %add_convert_fusion = bf16[2048,1536]{1,0:T(8,128)(2,1)} fusion(bf16[2048,1536]{1,0:T(8,128)(2,1)} %get-tuple-element.329.x_ref, bf16[2048,1536]{1,0:T(8,128)(2,1)} %get-tuple-element.332, bf16[1536,1536]{1,0:T(8,128)(2,1)} %all-gather.5.cloned.1.call-done), kind=kOutput, calls=%fused_computation.13 | convolution fusion | flops 9673113600 | bytes 23592960 | tf_op jit(solution)/shard_map/dot_general | solution.py:88
  795.3 66.9 %conditional.3 = (bf16[18992,1536]{1,0:T(8,128)(2,1)}) conditional(s32[]{:T(128)} %bitcast.10, (s32[]{:T(128)}, f32[8,176,1536]{2,1,0:T(8,128)}, s32[8,256]{1,0:T(8,128)S(1)}, s32[11,128]{1,0:T(8,128)S(1)}, s32[11,128]{1,0:T(8,128)S(1)}, /*index=5*/bf16[4096,1536]{1,0:T(8,128)(2,1)}) %tuple.115, (s32[8,2048]{1,0:T(8,128)}, s32[]{:T(128)}, ...), branch_computations={%region_5.6_spmd, %region_6.10_spmd} | conditional | flops 40000000000 | bytes 312185056 | solution.py:1033
  795.3 66.9 %final_rows.1 = bf16[18992,1536]{1,0:T(8,128)(2,1)} custom-call(s32[1]{0:T(128)} %bitcast.3.me_s, s32[8,256]{1,0:T(8,128)S(1)} %get-tuple-element.260.own_s, s32[11,128]{1,0:T(8,128)S(1)} %get-tuple-element.261.tgt_s, s32[11,128]{1,0:T(8,128)S(1)} %get-tuple-element.262.rep_s, bf16[4096,1536]{1,0:T(8,128)(2,1)} %get-tuple-element.263.hot_ref, ...), custom_call_target="tpu_custom_call" | custom-call | flops 40000000000 | bytes 80000000 | tf_op jit(solution)/shard_map/cond/branch_0_fun/final_rows/pallas_call | solution.py:866
  862.2 0.0 all-to-all-done.1
  862.2 0.7 reduce_sum.63
  863.0 0.6 fusion.7
  863.6 0.6 fusion.8
  864.2 2.4 slice.63
  866.6 1.8 fusion.4
  (20 shorter events, 0.1 us)
Async XLA Ops:
  7.2 213.7 %all-gather.5.cloned.1.call-start = ((), (), s32[]{:S(2)}) async-start(), calls=%async_computation.5 | async-start | bytes 5308416 | tf_op jit(solution)/shard_map/all_gather | solution.py:989
  9.4 226.6 %all-gather.3.cloned.1.call-start = ((), (), s32[]{:S(2)}) async-start(), calls=%async_computation.4 | async-start | bytes 7077888 | tf_op jit(solution)/shard_map/all_gather | solution.py:988
  136.6 27.9 %copy-start.5 = (s32[8,256]{1,0:T(8,128)}, s32[8,256]{1,0:T(8,128)S(1)}, u32[]{:S(2)}) copy-start(s32[8,256]{1,0:T(8,128)S(1)} %get-tuple-element.327.idx_s.idx_ref) | copy-start | bytes 24580
  164.5 9.2 %copy-start.2 = (f32[8,20,128]{2,1,0:T(8,128)S(1)}, f32[8,20,128]{2,1,0:T(8,128)}, u32[]{:S(2)}) copy-start(f32[8,20,128]{2,1,0:T(8,128)} %get-tuple-element.324) | copy-start | bytes 245764
  164.5 71.5 %all-to-all-start = ((bf16[8,176,1536]{2,1,0:T(8,128)(2,1)}), bf16[8,176,1536]{2,1,0:T(8,128)(2,1)}, u32[]{:S(2)}, u32[]{:S(2)}) async-start(bf16[8,176,1536]{2,1,0:T(8,128)(2,1)} %gather_rows.3), calls=%async_computation | async-start | bytes 8650752 | tf_op jit(solution)/shard_map/all_to_all | solution.py:1006
  171.8 692.4 %reduce-scatter.3.cloned.1.call-start = ((), (), s32[]{:S(2)}) async-start(), calls=%async_computation.6 | async-start | bytes 14155776 | tf_op jit(solution)/shard_map/reduce_scatter | solution.py:1021
  174.8 0.6 copy-start
  414.3 0.7 copy-start.6
  414.3 454.0 %reduce-scatter.5.cloned.1.call-start = ((), (), s32[]{:S(2)}) async-start(), calls=%async_computation.7 | async-start | bytes 10616832 | tf_op jit(solution)/shard_map/reduce_scatter | solution.py:1018
  420.1 23.8 %copy-start.4 = (f32[2,8,256]{2,1,0:T(8,128)S(1)}, f32[2,8,256]{2,1,0:T(8,128)}, u32[]{:S(2)}) copy-start(f32[2,8,256]{2,1,0:T(8,128)} %get-tuple-element.351) | copy-start | bytes 49156
  420.1 23.9 %copy-start.3 = (f32[2,8,256]{2,1,0:T(8,128)S(1)}, f32[2,8,256]{2,1,0:T(8,128)}, u32[]{:S(2)}) copy-start(f32[2,8,256]{2,1,0:T(8,128)} %get-tuple-element.352) | copy-start | bytes 49156
  420.1 24.0 %copy-start.1 = (f32[2,8,1536]{2,1,0:T(8,128)S(1)}, f32[2,8,1536]{2,1,0:T(8,128)}, u32[]{:S(2)}) copy-start(f32[2,8,1536]{2,1,0:T(8,128)} %get-tuple-element.350) | copy-start | bytes 294916
  445.8 416.4 %all-to-all-start.1 = ((f32[8,1,448]{2,1,0:T(1,128)}), f32[8,1,448]{2,1,0:T(1,128)}, u32[]{:S(2)}, u32[]{:S(2)}) async-start(f32[8,1,448]{2,1,0:T(1,128)} %all_to_all.10), calls=%async_computation.1 | async-start | bytes 32768 | tf_op jit(solution)/shard_map/all_to_all | solution.py:1027
  779.3 16.0 %copy-start.7 = (s32[8,256]{1,0:T(8,128)S(1)}, s32[8,256]{1,0:T(8,128)}, u32[]{:S(2)}) copy-start(s32[8,256]{1,0:T(8,128)} %copy-done.5) | copy-start | bytes 24580
Sparse Core Ops, SparseCore 0:
  9.8 39.7 all-gather.4
  51.9 52.3 all-gather.2
  414.4 143.3 reduce-scatter.2
  561.7 93.1 reduce-scatter.4
